TPU v7x, 16 devices: a 4x2x1 block of a 4x4x8 slice. The times are simulated.
16 devices in a mesh: data: 2 (over y, z), seq: 8 (over x, core).
Axes of the slice: x: 4, y: 2, z: 1, core: 2. Of those that a mesh axis runs over, the one named last changes fastest.
The devices are a block of a 4x4x8 slice.
Arguments:
- tokens: bfloat16 [16, 2048, 3072], P('data', 'seq'), parts along dimension 0
- theta_q: bfloat16 [3072, 3072], replicated
- theta_k: bfloat16 [3072, 3072], replicated
- theta_v: bfloat16 [3072, 3072], replicated
- w_out: bfloat16 [3072, 3072], replicated
- w_init: float32 [48, 64, 64], replicated
- inner_lr: float32 [48], replicated
Outputs:
- output: bfloat16 [16, 2048, 3072], P('data', 'seq'), parts along dimension 0
There are 2 independent parts. A program takes and returns all parts, laid end to end along the dimension named above; an argument that names none is the same for every part.
All inputs are finite; a program needn't handle non-finite values.
Results may differ from a plain program's by a relative error of at most 0.00243997.
Values are sent between devices in bfloat16 or wider.
A program may use at most 768 MiB of HBM per device.

v0:
```python
import jax
import jax.numpy as jnp
from jax import lax
from jax.sharding import PartitionSpec as P

MINI_BATCH = 16
FULL_PRECISION = lax.Precision.HIGHEST


def solution(mesh):
    group_size = mesh.shape["seq"]
    distances = [2 ** level for level in range(8) if 2 ** level < group_size]

    def per_device(tokens, theta_q, theta_k, theta_v, w_out, w_init, inner_lr):
        n_batch, tok_dev, width_d = tokens.shape
        n_heads, head_dim, _ = w_init.shape
        n_blocks = tok_dev // MINI_BATCH
        blocked = tokens.reshape(n_batch, n_blocks, MINI_BATCH, width_d)

        def project(theta):
            projected = jnp.einsum("bnsd,de->nbse", blocked, theta, preferred_element_type=jnp.float32)
            return projected.astype(jnp.bfloat16).reshape(n_blocks, n_batch, MINI_BATCH, n_heads, head_dim)

        step_size = ((2.0 / MINI_BATCH) * inner_lr)[None, :, None, None]
        eye_part = jnp.broadcast_to(jnp.eye(head_dim, dtype=jnp.float32), (n_batch, n_heads, head_dim, head_dim))
        zero_part = jnp.zeros_like(eye_part)

        def update(seg_map, block_in):
            q_blk, k_blk, v_blk = block_in
            k_map = jnp.einsum("bthd,bhde->bthe", k_blk, seg_map, precision=FULL_PRECISION, preferred_element_type=jnp.float32)
            residual = k_map - jnp.concatenate([jnp.zeros_like(v_blk), v_blk], axis=-1)
            gradient = jnp.einsum("bthd,bthe->bhde", k_blk, residual, precision=FULL_PRECISION, preferred_element_type=jnp.float32)
            seg_map = seg_map - step_size * gradient
            q_map = jnp.einsum("bthd,bhde->bthe", q_blk, seg_map, precision=FULL_PRECISION, preferred_element_type=jnp.float32)
            return seg_map, q_map

        seg_start = jnp.concatenate([eye_part, zero_part], axis=-1)
        seg_map, q_maps = lax.scan(update, seg_start, (project(theta_q), project(theta_k), project(theta_v)))
        my_index = lax.axis_index("seq")
        for distance in distances:
            received = lax.ppermute(seg_map, "seq", [(source, source + distance) for source in range(group_size - distance)])
            combined = jnp.einsum("bhde,bhef->bhdf", seg_map[..., :head_dim], received, precision=FULL_PRECISION, preferred_element_type=jnp.float32)
            combined = combined + jnp.concatenate([zero_part, seg_map[..., head_dim:]], axis=-1)
            seg_map = jnp.where(my_index >= distance, combined, seg_map)
        w_end = jnp.einsum("bhde,hef->bhdf", seg_map[..., :head_dim], w_init, precision=FULL_PRECISION, preferred_element_type=jnp.float32) + seg_map[..., head_dim:]
        w_prev = lax.ppermute(w_end, "seq", [(source, source + 1) for source in range(group_size - 1)])
        w_start = jnp.where(my_index == 0, w_init[None], w_prev)
        inner_out = jnp.einsum("nbthd,bhde->nbthe", q_maps[..., :head_dim], w_start, precision=FULL_PRECISION, preferred_element_type=jnp.float32) + q_maps[..., head_dim:]
        inner_out = inner_out.astype(jnp.bfloat16).reshape(n_blocks, n_batch, MINI_BATCH, n_heads * head_dim)
        result = jnp.einsum("nbsk,kd->bnsd", inner_out, w_out, preferred_element_type=jnp.float32)
        return result.astype(jnp.bfloat16).reshape(n_batch, tok_dev, width_d)

    tok_spec = P("data", "seq", None)
    return jax.shard_map(per_device, mesh=mesh, in_specs=(tok_spec, P(), P(), P(), P(), P(), P()), out_specs=tok_spec, check_vma=False)
```

profile of v0, /device:TPU:124, one launch (start us, length us, event | category | flops | bytes accessed | tf_op | source)
XLA Modules:
  0.0 1908.9 jit_solution(15309783313812606819)
XLA Ops:
  0.6 47.1 %convert_bitcast_fusion.3 = bf16[16,8,16,3072]{3,2,0,1:T(8,128)(2,1)} fusion(bf16[8,16,16,3072]{3,2,1,0:T(8,128)(2,1)} %bitcast.122, bf16[3072,3072]{1,0:T(8,128)(2,1)} %param.11), kind=kOutput, calls=%fused_computation.42 | convolution fusion | flops 38660997120 | bytes 44040192 | tf_op jit(solution)/shard_map/bnsd,de->nbse/dot_general | solution.py:21
  47.7 30.7 %reshape.20 = bf16[16,8,16,48,64]{4,3,2,0,1:T(8,128)(2,1)} reshape(bf16[16,8,16,3072]{3,2,0,1:T(8,128)(2,1)} %convert_bitcast_fusion.3) | data formatting | bytes 25165824 | tf_op jit(solution)/shard_map/reshape | solution.py:22
  78.4 47.5 %convert_bitcast_fusion.2 = bf16[16,8,16,3072]{3,2,0,1:T(8,128)(2,1)} fusion(bf16[8,16,16,3072]{3,2,1,0:T(8,128)(2,1)} %bitcast.123, bf16[3072,3072]{1,0:T(8,128)(2,1)} %param.12), kind=kOutput, calls=%fused_computation.41 | convolution fusion | flops 38660997120 | bytes 44040192 | tf_op jit(solution)/shard_map/bnsd,de->nbse/dot_general | solution.py:21
  125.9 30.7 %reshape.21 = bf16[16,8,16,48,64]{4,3,2,0,1:T(8,128)(2,1)} reshape(bf16[16,8,16,3072]{3,2,0,1:T(8,128)(2,1)} %convert_bitcast_fusion.2) | data formatting | bytes 25165824 | tf_op jit(solution)/shard_map/reshape | solution.py:22
  156.5 47.2 %convert_bitcast_fusion.1 = bf16[16,8,16,3072]{3,2,0,1:T(8,128)(2,1)} fusion(bf16[8,16,16,3072]{3,2,1,0:T(8,128)(2,1)} %bitcast.124, bf16[3072,3072]{1,0:T(8,128)(2,1)} %param.10), kind=kOutput, calls=%fused_computation.40 | convolution fusion | flops 38660997120 | bytes 44040192 | tf_op jit(solution)/shard_map/bnsd,de->nbse/dot_general | solution.py:21
  203.7 30.7 %reshape.22 = bf16[16,8,16,48,64]{4,3,2,0,1:T(8,128)(2,1)} reshape(bf16[16,8,16,3072]{3,2,0,1:T(8,128)(2,1)} %convert_bitcast_fusion.1) | data formatting | bytes 25165824 | tf_op jit(solution)/shard_map/reshape | solution.py:22
  240.8 12.0 concatenate.15
  252.8 535.0 %while.12 = (s32[]{:T(128)}, f32[8,48,64,128]{3,2,1,0:T(8,128)}, f32[16,8,16,48,128]{4,2,0,3,1:T(8,128)}, f32[1,48,1,1]{1,3,2,0:T(1,128)S(1)}, bf16[16,8,16,48,6...) while((s32[]{:T(128)}, f32[8,48,64,128]{3,2,1,0:T(8,128)}, ...), condition=%wide.region_1.2_spmd, body=%wide.region_0.1_spmd.sunk | while | flops 1819803648 | bytes 169870160 | solution.py:38
  789.8 12.7 slice.31
  802.5 125.1 %collective-permute-done = f32[8,48,64,128]{3,2,1,0:T(8,128)} collective-permute-done((f32[8,48,64,128]{3,2,1,0:T(8,128)}, f32[8,48,64,128]{3,2,1,0:T(8,128)}, u32[]{:S(2)}, u32[]{:S(2)}) %collective-permute-start) | collective-permute-done | bytes 12582944 | tf_op jit(solution)/shard_map/ppermute | solution.py:41
  927.6 27.2 %add_select_fusion.2 = f32[8,48,64,128]{3,2,1,0:T(8,128)} fusion(f32[8,48,64,128]{3,2,1,0:T(8,128)} %get-tuple-element.43, f32[8,48,64,64]{3,2,1,0:T(8,128)} %slice.31, pred[]{:T(512)S(6)} %ge.11, f32[8,48,64,128]{3,2,1,0:T(8,128)} %collective-permute-done), kind=kOutput, calls=%fused_computation.37 | convolution fusion | flops 2422210560 | bytes 62914560 | tf_op jit(solution)/shard_map/bhde,bhef->bhdf/dot_general | solution.py:42
  958.3 12.7 slice.41
  970.9 257.0 %collective-permute-done.1 = f32[8,48,64,128]{3,2,1,0:T(8,128)} collective-permute-done((f32[8,48,64,128]{3,2,1,0:T(8,128)}, f32[8,48,64,128]{3,2,1,0:T(8,128)}, u32[]{:S(2)}, u32[]{:S(2)}) %collective-permute-start.1) | collective-permute-done | bytes 12582944 | tf_op jit(solution)/shard_map/ppermute | solution.py:41
  1227.9 27.0 %add_select_fusion.1 = f32[8,48,64,128]{3,2,1,0:T(8,128)} fusion(f32[8,48,64,128]{3,2,1,0:T(8,128)} %add_select_fusion.2, f32[8,48,64,64]{3,2,1,0:T(8,128)} %slice.41, pred[]{:T(512)S(6)} %ge.10, f32[8,48,64,128]{3,2,1,0:T(8,128)} %collective-permute-done.1), kind=kOutput, calls=%fused_computation.36 | convolution fusion | flops 2422210560 | bytes 62914560 | tf_op jit(solution)/shard_map/bhde,bhef->bhdf/dot_general | solution.py:42
  1256.6 12.7 slice.43
  1269.3 259.7 %collective-permute-done.2 = f32[8,48,64,128]{3,2,1,0:T(8,128)} collective-permute-done((f32[8,48,64,128]{3,2,1,0:T(8,128)}, f32[8,48,64,128]{3,2,1,0:T(8,128)}, u32[]{:S(2)}, u32[]{:S(2)}) %collective-permute-start.2) | collective-permute-done | bytes 12582944 | tf_op jit(solution)/shard_map/ppermute | solution.py:41
  1529.0 27.1 %add_select_fusion = f32[8,48,64,128]{3,2,1,0:T(8,128)} fusion(f32[8,48,64,128]{3,2,1,0:T(8,128)} %add_select_fusion.1, f32[8,48,64,64]{3,2,1,0:T(8,128)} %slice.43, pred[]{:T(512)S(6)} %ge.9, f32[8,48,64,128]{3,2,1,0:T(8,128)} %collective-permute-done.2), kind=kOutput, calls=%fused_computation.35 | convolution fusion | flops 2422210560 | bytes 62914560 | tf_op jit(solution)/shard_map/bhde,bhef->bhdf/dot_general | solution.py:42
  1556.1 17.8 slice_add_fusion
  1575.9 137.8 %collective-permute-done.3 = f32[8,48,64,64]{3,2,1,0:T(8,128)} collective-permute-done((f32[8,48,64,64]{3,2,1,0:T(8,128)}, f32[8,48,64,64]{3,2,1,0:T(8,128)}, u32[]{:S(2)}, u32[]{:S(2)}) %collective-permute-start.3) | collective-permute-done | bytes 6291488 | tf_op jit(solution)/shard_map/ppermute | solution.py:46
  1713.6 64.4 %fusion.4 = bf16[16,8,16,48,64]{4,2,0,3,1:T(8,128)(2,1)} fusion(f32[16,8,16,48,128]{4,2,0,3,1:T(8,128)} %get-tuple-element.44, f32[8,48,64,64]{3,2,1,0:T(8,128)} %collective-permute-done.3, f32[48,64,64]{2,1,0:T(8,128)S(1)} %copy-done.2, pred[]{:T(512)S(6)} %eq.6), kind=kOutput, calls=%fused_computation.14 | convolution fusion | flops 4845993984 | bytes 126615552 | tf_op jit(solution)/shard_map/nbthd,bhde->nbthe/dot_general | solution.py:48
  1778.0 41.3 %copy.18 = bf16[16,8,16,48,64]{4,3,2,1,0:T(8,128)(2,1)} copy(bf16[16,8,16,48,64]{4,2,0,3,1:T(8,128)(2,1)} %fusion.4) | data formatting | bytes 25165824 | tf_op jit(solution)/shard_map/convert_element_type | solution.py:49
  1819.3 31.4 %reshape.23 = bf16[16,8,16,3072]{3,2,1,0:T(8,128)(2,1)} reshape(bf16[16,8,16,48,64]{4,3,2,1,0:T(8,128)(2,1)} %copy.18) | data formatting | bytes 25165824 | tf_op jit(solution)/shard_map/reshape | solution.py:49
  1850.7 47.0 %convert_bitcast_fusion = bf16[8,16,16,3072]{3,2,0,1:T(8,128)(2,1)} fusion(bf16[16,8,16,3072]{3,2,1,0:T(8,128)(2,1)} %reshape.23, bf16[3072,3072]{1,0:T(8,128)(2,1)} %param.13), kind=kOutput, calls=%fused_computation.33 | convolution fusion | flops 38660997120 | bytes 44040192 | tf_op jit(solution)/shard_map/nbsk,kd->bnsd/dot_general | solution.py:50
  1897.8 10.9 copy.19
  (174 shorter events, 550.0 us)
Async XLA Ops:
  203.7 30.7 %copy-start.4 = (f32[48]{0:T(128)S(1)}, f32[48]{0:T(128)}, u32[]{:S(2)}) copy-start(f32[48]{0:T(128)} %param.15) | copy-start | bytes 580
  203.7 30.7 %copy-start.3 = (f32[64,64]{1,0:T(8,128)S(1)}, f32[64,64]{1,0:T(8,128)}, u32[]{:S(2)}) copy-start(f32[64,64]{1,0:T(8,128)} %fusion.46) | copy-start | bytes 49156
  253.2 6.0 copy-start
  274.4 4.5 copy-start.1
  286.6 6.0 copy-start
  320.0 6.0 copy-start
  353.4 6.0 copy-start
  386.8 6.0 copy-start
  420.1 6.0 copy-start
  453.5 6.0 copy-start
  487.0 6.0 copy-start
  520.4 6.0 copy-start
  553.7 6.0 copy-start
  587.1 6.0 copy-start
  620.6 6.0 copy-start
  654.1 6.0 copy-start
  687.5 6.0 copy-start
  721.0 6.0 copy-start
  754.4 6.0 copy-start
  787.9 139.7 %collective-permute-start = (f32[8,48,64,128]{3,2,1,0:T(8,128)}, f32[8,48,64,128]{3,2,1,0:T(8,128)}, u32[]{:S(2)}, u32[]{:S(2)}) collective-permute-start(f32[8,48,64,128]{3,2,1,0:T(8,128)} %get-tuple-element.43), channel_id=1, source_target_pairs={{0,1},{1,2},{2,3},{3,4},{4,5},{5,6},{6,7},{8,9},{9,10},{10,11},{11... | collective-permute-start | bytes 37748744 | tf_op jit(solution)/shard_map/ppermute | solution.py:41
  954.8 273.1 %collective-permute-start.1 = (f32[8,48,64,128]{3,2,1,0:T(8,128)}, f32[8,48,64,128]{3,2,1,0:T(8,128)}, u32[]{:S(2)}, u32[]{:S(2)}) collective-permute-start(f32[8,48,64,128]{3,2,1,0:T(8,128)} %add_select_fusion.2), channel_id=1, source_target_pairs={{0,2},{1,3},{2,4},{3,5},{4,6},{5,7},{8,10},{9,11},{10,12},{11,13},... | collective-permute-start | bytes 37748744 | tf_op jit(solution)/shard_map/ppermute | solution.py:41
  1254.9 274.1 %collective-permute-start.2 = (f32[8,48,64,128]{3,2,1,0:T(8,128)}, f32[8,48,64,128]{3,2,1,0:T(8,128)}, u32[]{:S(2)}, u32[]{:S(2)}) collective-permute-start(f32[8,48,64,128]{3,2,1,0:T(8,128)} %add_select_fusion.1), channel_id=1, source_target_pairs={{0,4},{1,5},{2,6},{3,7},{8,12},{9,13},{10,14},{11,15}} | collective-permute-start | bytes 37748744 | tf_op jit(solution)/shard_map/ppermute | solution.py:41
  1269.3 286.8 %copy-start.2 = (f32[48,64,64]{2,1,0:T(8,128)S(1)}, f32[48,64,64]{2,1,0:T(8,128)}, u32[]{:S(2)}) copy-start(f32[48,64,64]{2,1,0:T(8,128)} %param.14) | copy-start | bytes 2359300
  1573.9 139.7 %collective-permute-start.3 = (f32[8,48,64,64]{3,2,1,0:T(8,128)}, f32[8,48,64,64]{3,2,1,0:T(8,128)}, u32[]{:S(2)}, u32[]{:S(2)}) collective-permute-start(f32[8,48,64,64]{3,2,1,0:T(8,128)} %slice_add_fusion), channel_id=1, source_target_pairs={{0,1},{1,2},{2,3},{3,4},{4,5},{5,6},{6,7},{8,9},{9,10},{10,11},{11... | collective-permute-start | bytes 18874376 | tf_op jit(solution)/shard_map/ppermute | solution.py:46
  (15 other events, 67.0 us)
where the time goes:
time: 1920 us; the launch traced here: 1910 us
  waiting for transfers between devices  780 us (41%)
  matrix products  719 us (37%)
  local copies, waits for them, and re-layouts  399 us (21%)
    ppermute x3, waiting for transfers between devices, per_device(): lax.ppermute(seg_map, 'seq', [(source, source + distance) for source in r...  642 us
    dot_general x16, matrix products, update(): jnp.einsum('bthd,bthe->bhde', k_blk, residual, precision=FULL_PRECISION,...  142 us
    dot_general x3, matrix products, project(): jnp.einsum('bnsd,de->nbse', blocked, theta, preferred_element_type=jnp.fl...  142 us
    ppermute x1, waiting for transfers between devices, per_device(): lax.ppermute(w_end, 'seq', [(source, source + 1) for source in range(grou...  138 us
    dot_general x16, matrix products, update(): jnp.einsum('bthd,bhde->bthe', q_blk, seg_map, precision=FULL_PRECISION, p...  124 us
    dot_general x16, matrix products, update(): jnp.einsum('bthd,bhde->bthe', k_blk, seg_map, precision=FULL_PRECISION, p...  101 us
    reshape x3, local copies, waits for them, and re-layouts, project(): projected.astype(jnp.bfloat16)  92.1 us
    while x64, local copies, waits for them, and re-layouts  84.8 us
  transfers between devices with their start and end apart: 4, of which 4 were waited for; matrix products, arithmetic and copies ran while one was open for 2% of the time, Pallas kernels for 0%

commit v1 on v0

v1 whole, which is shorter than its diff:
```python
import functools

import jax
import jax.numpy as jnp
from jax import lax
from jax.experimental import pallas as pl
from jax.experimental.pallas import tpu as pltpu
from jax.sharding import PartitionSpec as P

MINI_BATCH = 16
HEADS_PER_GROUP = 4
STEPS_PER_TRIP = 5
bf16, f32 = jnp.bfloat16, jnp.float32


def split3(x):
    a = x.astype(bf16)
    rest = x - a.astype(f32)
    b = rest.astype(bf16)
    return a, b, (rest - b.astype(f32)).astype(bf16)


def per_head_rows(x, low):
    rows = []
    for half in range(2):
        y = x[:, half * 128:(half + 1) * 128]
        turned = pltpu.roll(y, 64, 1)
        rows += [jnp.where(low, y, turned), jnp.where(low, turned, y)]
    return rows


def own_columns(z, low, first):
    t = MINI_BATCH
    return jnp.concatenate([
        jnp.where(low, z[first:first + t, :128], z[first + t:first + 2 * t, :128]),
        jnp.where(low, z[first + 2 * t:first + 3 * t, 128:], z[first + 3 * t:first + 4 * t, 128:])], axis=1)


def times_w(rows, w):
    m = jnp.concatenate(rows, axis=0)
    lhs = jnp.concatenate([m, m], axis=1)
    rhs = jnp.concatenate([*split3(w), jnp.zeros(w.shape, bf16)], axis=0)
    return jnp.dot(lhs, rhs, preferred_element_type=f32)


def k_transposed_times(k_rows, r, low):
    zero = jnp.zeros((MINI_BATCH, 128), bf16)
    rows = []
    for part in split3(r):
        a, b = part[:, :128], part[:, 128:]
        rows += [jnp.concatenate([jnp.where(low, a, zero), zero], axis=1), jnp.concatenate([jnp.where(low, zero, a), zero], axis=1),
                 jnp.concatenate([zero, jnp.where(low, b, zero)], axis=1), jnp.concatenate([zero, jnp.where(low, zero, b)], axis=1)]
    rhs = jnp.concatenate([*rows, jnp.zeros((4 * MINI_BATCH, 256), bf16)], axis=0)
    k_mat = jnp.concatenate(k_rows, axis=0)
    turned = jnp.concatenate([k_mat, k_mat], axis=0).T[:64]
    lhs = jnp.concatenate([turned, turned], axis=1)
    return jnp.dot(lhs, rhs, preferred_element_type=f32)


def inner_kernel(n_seq, n_batch, tok_dev, n_groups, q_hbm, k_hbm, v_hbm, w_init_ref, eta_ref, o_hbm,
                 q_buf, k_buf, v_buf, w_buf, in_sem, out_sem, send_sem, recv_sem):
    me = lax.axis_index("seq")
    barrier = pltpu.get_barrier_semaphore()

    def columns(g):
        return pl.ds(pl.multiple_of(g * 256, 256), 256)

    def loads(g):
        slot = lax.rem(g, 2)
        return [pltpu.make_async_copy(hbm.at[:, columns(g)], buf.at[slot], in_sem.at[i, slot])
                for i, (hbm, buf) in enumerate(((q_hbm, q_buf), (k_hbm, k_buf), (v_hbm, v_buf)))]

    def result(g):
        slot = lax.rem(g, 2)
        return pltpu.make_async_copy(q_buf.at[slot], o_hbm.at[:, columns(g)], out_sem.at[slot])

    def hand_on(g):
        return pltpu.make_async_remote_copy(w_buf.at[g], w_buf.at[g], send_sem.at[g], recv_sem.at[g],
                                            device_id={"seq": lax.rem(me + 1, n_seq)}, device_id_type=pl.DeviceIdType.MESH)

    for copy in loads(0):
        copy.start()

    for peer in (lax.rem(me + 1, n_seq), lax.rem(me + n_seq - 1, n_seq)):
        pl.semaphore_signal(barrier, inc=1, device_id={"seq": peer}, device_id_type=pl.DeviceIdType.MESH)
    pl.semaphore_wait(barrier, 2)

    low = lax.broadcasted_iota(jnp.int32, (MINI_BATCH, 128), 1) < 64
    n_steps = tok_dev // MINI_BATCH

    def group(g, _):
        slot = lax.rem(g, 2)

        @pl.when(g >= 1)
        def _():
            result(g - 1).wait()

        @pl.when(g + 1 < n_groups)
        def _():
            for copy in loads(g + 1):
                copy.start()

        for copy in loads(g):
            copy.wait()

        @pl.when(me == 0)
        def _():
            for b in range(n_batch):
                w_buf[g, b] = w_init_ref[g]

        @pl.when(me > 0)
        def _():
            hand_on(g).wait_recv()

        eta = eta_ref[g]

        def rows_of(b, j):
            start = b * tok_dev + j * MINI_BATCH
            return pl.ds(start if isinstance(start, int) else pl.multiple_of(start, MINI_BATCH), MINI_BATCH)

        def step(j, with_k, with_q):
            k_rows, z = {}, {}
            for b in range(n_batch):
                rows = []
                if with_k:
                    k_rows[b] = per_head_rows(k_buf[slot, rows_of(b, j), :], low)
                    rows += k_rows[b]
                if with_q:
                    rows += per_head_rows(q_buf[slot, rows_of(b, j - 1), :], low)
                prod = times_w(rows, w_buf[g, b])
                if with_k:
                    z[b] = own_columns(prod, low, 0)
                if with_q:
                    q_buf[slot, rows_of(b, j - 1), :] = own_columns(prod, low, 4 * MINI_BATCH if with_k else 0).astype(bf16)
            if with_k:
                for b in range(n_batch):
                    r = (z[b] - v_buf[slot, rows_of(b, j), :].astype(f32)) * eta
                    w_buf[g, b] -= k_transposed_times(k_rows[b], r, low)

        step(0, True, False)

        def trip(i, _):
            for s in range(STEPS_PER_TRIP):
                step(1 + i * STEPS_PER_TRIP + s, True, True)
            return 0

        lax.fori_loop(0, (n_steps - 1) // STEPS_PER_TRIP, trip, 0)

        @pl.when(me < n_seq - 1)
        def _():
            hand_on(g).start()

        step(n_steps, False, True)
        result(g).start()
        return 0

    lax.fori_loop(0, n_groups, group, 0)
    result(n_groups - 1).wait()

    @pl.when(me < n_seq - 1)
    def _():
        for g in range(n_groups):
            hand_on(g).wait_send()


def solution(mesh):
    n_seq = mesh.shape["seq"]

    def per_device(tokens, theta_q, theta_k, theta_v, w_out, w_init, inner_lr):
        n_batch, tok_dev, width_d = tokens.shape
        n_heads, head_dim, _ = w_init.shape
        n_groups = n_heads // HEADS_PER_GROUP
        n_rows, width = n_batch * tok_dev, n_heads * head_dim
        flat = tokens.reshape(n_rows, width_d)
        q, k, v = (jnp.dot(flat, theta, preferred_element_type=f32).astype(bf16) for theta in (theta_q, theta_k, theta_v))
        w_start = w_init.reshape(n_groups, HEADS_PER_GROUP, head_dim, head_dim).transpose(0, 2, 1, 3).reshape(n_groups, head_dim, 4 * head_dim)
        eta = jnp.repeat((2.0 / MINI_BATCH) * inner_lr, head_dim).reshape(n_groups, 1, 4 * head_dim)
        hbm, vmem = pl.BlockSpec(memory_space=pl.ANY), pl.BlockSpec(memory_space=pltpu.VMEM)
        slab = pltpu.VMEM((2, n_rows, 4 * head_dim), bf16)
        o = pl.pallas_call(
            functools.partial(inner_kernel, n_seq, n_batch, tok_dev, n_groups),
            out_shape=jax.ShapeDtypeStruct((n_rows, width), bf16),
            in_specs=[hbm, hbm, hbm, vmem, vmem], out_specs=hbm,
            scratch_shapes=[slab, slab, slab, pltpu.VMEM((n_groups, n_batch, head_dim, 4 * head_dim), f32),
                            pltpu.SemaphoreType.DMA((3, 2)), pltpu.SemaphoreType.DMA((2,)),
                            pltpu.SemaphoreType.DMA((n_groups,)), pltpu.SemaphoreType.DMA((n_groups,))],
            compiler_params=pltpu.CompilerParams(collective_id=0, has_side_effects=True, vmem_limit_bytes=48 * 1024 * 1024),
            name="inner",
        )(q, k, v, w_start, eta)
        result = jnp.dot(o, w_out, preferred_element_type=f32).astype(bf16)
        return result.reshape(n_batch, tok_dev, width_d)

    tok_spec = P("data", "seq", None)
    return jax.shard_map(per_device, mesh=mesh, in_specs=(tok_spec, P(), P(), P(), P(), P(), P()), out_specs=tok_spec, check_vma=False)
```

time: 1920 us -> 730 us (0.38)
  the two profiles are of different devices: /device:TPU:124 before, /device:TPU:127 now
where the time goes in v1:
time: 730 us
  Pallas kernels  538 us (74%)
  matrix products  187 us (26%)
    pallas_call x1, Pallas kernels, per_device(): pl.pallas_call(functools.partial(inner_kernel, n_seq, n_batch, tok_dev, n...  538 us
    dot_general x3, matrix products, per_device(): jnp.dot(flat, theta, preferred_element_type=f32).astype(bf16)  140 us
    dot_general x1, matrix products, per_device(): result = jnp.dot(o, w_out, preferred_element_type=f32).astype(bf16)  47 us

profile of v1, /device:TPU:127, one launch (start us, length us, event | category | flops | bytes accessed | tf_op | source)
XLA Modules:
  0.0 729.6 jit_solution(12861650548083898391)
XLA Ops:
  0.0 0.7 broadcast_multiply_fusion
  0.7 0.1 broadcast_in_dim.7
  0.7 0.1 broadcast_in_dim.8
  0.8 0.1 broadcast_in_dim.9.eta_ref
  0.9 2.4 copy.11
  3.4 0.9 reshape.21.w_init_ref
  4.2 46.8 %convolution_convert_fusion.1.v_hbm = bf16[2048,3072]{1,0:T(8,128)(2,1)} fusion(bf16[2048,3072]{1,0:T(8,128)(2,1)} %bitcast.16, bf16[3072,3072]{1,0:T(8,128)(2,1)} %param.10), kind=kOutput, calls=%fused_computation.1 | convolution fusion | flops 38660997120 | bytes 44040192 | tf_op jit(solution)/shard_map/dot_general | solution.py:175
  51.0 46.9 %convolution_convert_fusion.2.k_hbm = bf16[2048,3072]{1,0:T(8,128)(2,1)} fusion(bf16[2048,3072]{1,0:T(8,128)(2,1)} %bitcast.17, bf16[3072,3072]{1,0:T(8,128)(2,1)} %param.9), kind=kOutput, calls=%fused_computation.2 | convolution fusion | flops 38660997120 | bytes 44040192 | tf_op jit(solution)/shard_map/dot_general | solution.py:175
  97.9 46.7 %convolution_convert_fusion.3.q_hbm = bf16[2048,3072]{1,0:T(8,128)(2,1)} fusion(bf16[2048,3072]{1,0:T(8,128)(2,1)} %bitcast.18, bf16[3072,3072]{1,0:T(8,128)(2,1)} %param.8), kind=kOutput, calls=%fused_computation.3 | convolution fusion | flops 38660997120 | bytes 44040192 | tf_op jit(solution)/shard_map/dot_general | solution.py:175
  144.6 538.0 %inner.1 = bf16[2048,3072]{1,0:T(8,128)(2,1)} custom-call(bf16[2048,3072]{1,0:T(8,128)(2,1)} %convolution_convert_fusion.3.q_hbm, bf16[2048,3072]{1,0:T(8,128)(2,1)} %convolution_convert_fusion.2.k_hbm, bf16[2048,3072]{1,0:T(8,128)(2,1)} %convolution_convert_fusion.1.v_hbm, f32[12,64,256]{2,1,0:T(8,128)S(1)} %reshape.21.w_init_ref, ...), custom_call_target="tpu_custom_call" | custom-call | tf_op jit(solution)/shard_map/inner/pallas_call | solution.py:180
  682.7 47.0 %convolution_convert_fusion = bf16[2048,3072]{1,0:T(8,128)(2,1)} fusion(bf16[2048,3072]{1,0:T(8,128)(2,1)} %inner.1, bf16[3072,3072]{1,0:T(8,128)(2,1)} %param.11), kind=kOutput, calls=%fused_computation | convolution fusion | flops 38660997120 | bytes 44040192 | tf_op jit(solution)/shard_map/dot_general | solution.py:190

commit v2 on v1

--- a/solution.py
+++ b/solution.py
@@ -58,7 +58,7 @@
 
 
 def inner_kernel(n_seq, n_batch, tok_dev, n_groups, q_hbm, k_hbm, v_hbm, w_init_ref, eta_ref, o_hbm,
-                 q_buf, k_buf, v_buf, w_buf, in_sem, out_sem, send_sem, recv_sem):
+                 q_buf, k_buf, v_buf, w_buf, w_now, in_sem, out_sem, send_sem, recv_sem):
     me = lax.axis_index("seq")
     barrier = pltpu.get_barrier_semaphore()
 
@@ -106,11 +106,12 @@
         @pl.when(me == 0)
         def _():
             for b in range(n_batch):
-                w_buf[g, b] = w_init_ref[g]
+                w_now[b] = w_init_ref[g]
 
         @pl.when(me > 0)
         def _():
             hand_on(g).wait_recv()
+            w_now[...] = w_buf[g]
 
         eta = eta_ref[g]
 
@@ -119,23 +120,24 @@
             return pl.ds(start if isinstance(start, int) else pl.multiple_of(start, MINI_BATCH), MINI_BATCH)
 
         def step(j, with_k, with_q):
-            k_rows, z = {}, {}
+            k_rows, rows, z = {}, {}, {}
             for b in range(n_batch):
-                rows = []
+                rows[b] = []
                 if with_k:
                     k_rows[b] = per_head_rows(k_buf[slot, rows_of(b, j), :], low)
-                    rows += k_rows[b]
+                    rows[b] += k_rows[b]
                 if with_q:
-                    rows += per_head_rows(q_buf[slot, rows_of(b, j - 1), :], low)
-                prod = times_w(rows, w_buf[g, b])
-                if with_k:
-                    z[b] = own_columns(prod, low, 0)
-                if with_q:
-                    q_buf[slot, rows_of(b, j - 1), :] = own_columns(prod, low, 4 * MINI_BATCH if with_k else 0).astype(bf16)
+                    rows[b] += per_head_rows(q_buf[slot, rows_of(b, j - 1), :], low)
+            prod = {b: times_w(rows[b], w_now[b]) for b in range(n_batch)}
+            if with_k:
+                z = {b: own_columns(prod[b], low, 0) for b in range(n_batch)}
+            if with_q:
+                for b in range(n_batch):
+                    q_buf[slot, rows_of(b, j - 1), :] = own_columns(prod[b], low, 4 * MINI_BATCH if with_k else 0).astype(bf16)
             if with_k:
                 for b in range(n_batch):
                     r = (z[b] - v_buf[slot, rows_of(b, j), :].astype(f32)) * eta
-                    w_buf[g, b] -= k_transposed_times(k_rows[b], r, low)
+                    w_now[b] -= k_transposed_times(k_rows[b], r, low)
 
         step(0, True, False)
 
@@ -148,6 +150,7 @@
 
         @pl.when(me < n_seq - 1)
         def _():
+            w_buf[g] = w_now[...]
             hand_on(g).start()
 
         step(n_steps, False, True)
@@ -182,6 +185,7 @@
             out_shape=jax.ShapeDtypeStruct((n_rows, width), bf16),
             in_specs=[hbm, hbm, hbm, vmem, vmem], out_specs=hbm,
             scratch_shapes=[slab, slab, slab, pltpu.VMEM((n_groups, n_batch, head_dim, 4 * head_dim), f32),
+                            pltpu.VMEM((n_batch, head_dim, 4 * head_dim), f32),
                             pltpu.SemaphoreType.DMA((3, 2)), pltpu.SemaphoreType.DMA((2,)),
                             pltpu.SemaphoreType.DMA((n_groups,)), pltpu.SemaphoreType.DMA((n_groups,))],
             compiler_params=pltpu.CompilerParams(collective_id=0, has_side_effects=True, vmem_limit_bytes=48 * 1024 * 1024),

time: 730 us -> 368 us (0.50)
  Pallas kernels: 538 us -> 177 us
    pallas_call x1, Pallas kernels: 538 us -> 177 us  [per_device(): pl.pallas_call(functools.partial(inner_kernel, n_seq, n_batch, tok_dev, n...]
where the time goes in v2:
time: 368 us
  matrix products  187 us (51%)
  Pallas kernels  177 us (48%)
    pallas_call x1, Pallas kernels, per_device(): pl.pallas_call(functools.partial(inner_kernel, n_seq, n_batch, tok_dev, n...  177 us
    dot_general x3, matrix products, per_device(): jnp.dot(flat, theta, preferred_element_type=f32).astype(bf16)  140 us
    dot_general x1, matrix products, per_device(): result = jnp.dot(o, w_out, preferred_element_type=f32).astype(bf16)  47 us

profile of v2, /device:TPU:127, one launch (start us, length us, event | category | flops | bytes accessed | tf_op | source)
XLA Modules:
  0.0 368.3 jit_solution(11612693122341338703)
XLA Ops:
  0.0 0.7 broadcast_multiply_fusion
  0.7 0.1 broadcast_in_dim.7
  0.7 0.1 broadcast_in_dim.8
  0.8 0.1 broadcast_in_dim.9.eta_ref
  0.9 2.4 copy.11
  3.4 0.9 reshape.21.w_init_ref
  4.2 46.8 %convolution_convert_fusion.1.v_hbm = bf16[2048,3072]{1,0:T(8,128)(2,1)} fusion(bf16[2048,3072]{1,0:T(8,128)(2,1)} %bitcast.16, bf16[3072,3072]{1,0:T(8,128)(2,1)} %param.10), kind=kOutput, calls=%fused_computation.1 | convolution fusion | flops 38660997120 | bytes 44040192 | tf_op jit(solution)/shard_map/dot_general | solution.py:178
  51.0 46.9 %convolution_convert_fusion.2.k_hbm = bf16[2048,3072]{1,0:T(8,128)(2,1)} fusion(bf16[2048,3072]{1,0:T(8,128)(2,1)} %bitcast.17, bf16[3072,3072]{1,0:T(8,128)(2,1)} %param.9), kind=kOutput, calls=%fused_computation.2 | convolution fusion | flops 38660997120 | bytes 44040192 | tf_op jit(solution)/shard_map/dot_general | solution.py:178
  97.9 46.7 %convolution_convert_fusion.3.q_hbm = bf16[2048,3072]{1,0:T(8,128)(2,1)} fusion(bf16[2048,3072]{1,0:T(8,128)(2,1)} %bitcast.18, bf16[3072,3072]{1,0:T(8,128)(2,1)} %param.8), kind=kOutput, calls=%fused_computation.3 | convolution fusion | flops 38660997120 | bytes 44040192 | tf_op jit(solution)/shard_map/dot_general | solution.py:178
  144.6 176.7 %inner.1 = bf16[2048,3072]{1,0:T(8,128)(2,1)} custom-call(bf16[2048,3072]{1,0:T(8,128)(2,1)} %convolution_convert_fusion.3.q_hbm, bf16[2048,3072]{1,0:T(8,128)(2,1)} %convolution_convert_fusion.2.k_hbm, bf16[2048,3072]{1,0:T(8,128)(2,1)} %convolution_convert_fusion.1.v_hbm, f32[12,64,256]{2,1,0:T(8,128)S(1)} %reshape.21.w_init_ref, ...), custom_call_target="tpu_custom_call" | custom-call | tf_op jit(solution)/shard_map/inner/pallas_call | solution.py:183
  321.4 47.0 %convolution_convert_fusion = bf16[2048,3072]{1,0:T(8,128)(2,1)} fusion(bf16[2048,3072]{1,0:T(8,128)(2,1)} %inner.1, bf16[3072,3072]{1,0:T(8,128)(2,1)} %param.11), kind=kOutput, calls=%fused_computation | convolution fusion | flops 38660997120 | bytes 44040192 | tf_op jit(solution)/shard_map/dot_general | solution.py:194

commit v3 on v2

v3 whole, which is shorter than its diff:
```python
import functools

import jax
import jax.numpy as jnp
from jax import lax
from jax.experimental import pallas as pl
from jax.experimental.pallas import tpu as pltpu
from jax.sharding import PartitionSpec as P

MINI_BATCH = 16
HEADS_PER_GROUP = 4
STEPS_PER_TRIP = 15
bf16, f32 = jnp.bfloat16, jnp.float32


def split3(x):
    a = x.astype(bf16)
    rest = x - a.astype(f32)
    b = rest.astype(bf16)
    return a, b, (rest - b.astype(f32)).astype(bf16)


def per_head_rows(x, low):
    rows = []
    for half in range(2):
        y = x[:, half * 128:(half + 1) * 128]
        turned = pltpu.roll(y, 64, 1)
        rows += [jnp.where(low, y, turned), jnp.where(low, turned, y)]
    return rows


def own_columns(z, low, first):
    t = MINI_BATCH
    return jnp.concatenate([
        jnp.where(low, z[first:first + t, :128], z[first + t:first + 2 * t, :128]),
        jnp.where(low, z[first + 2 * t:first + 3 * t, 128:], z[first + 3 * t:first + 4 * t, 128:])], axis=1)


def times_w(rows, w):
    m = jnp.concatenate(rows, axis=0)
    lhs = jnp.concatenate([m, m], axis=1)
    rhs = jnp.concatenate([*split3(w), jnp.zeros(w.shape, bf16)], axis=0)
    return jnp.dot(lhs, rhs, preferred_element_type=f32)


def k_transposed_times(k_rows, r, low):
    zero = jnp.zeros((MINI_BATCH, 128), bf16)
    rows = []
    for part in split3(r):
        a, b = part[:, :128], part[:, 128:]
        rows += [jnp.concatenate([jnp.where(low, a, zero), zero], axis=1), jnp.concatenate([jnp.where(low, zero, a), zero], axis=1),
                 jnp.concatenate([zero, jnp.where(low, b, zero)], axis=1), jnp.concatenate([zero, jnp.where(low, zero, b)], axis=1)]
    rhs = jnp.concatenate([*rows, jnp.zeros((4 * MINI_BATCH, 256), bf16)], axis=0)
    k_mat = jnp.concatenate(k_rows, axis=0)
    turned = jnp.concatenate([k_mat, k_mat], axis=0).T[:64]
    lhs = jnp.concatenate([turned, turned], axis=1)
    return jnp.dot(lhs, rhs, preferred_element_type=f32)


def fused_kernel(n_seq, n_batch, tok_dev, n_groups, x_hbm, theta_k_hbm, theta_v_hbm, theta_q_hbm, w_init_hbm, eta_ref, o_hbm,
                 x_buf, kvq_buf, theta_buf, tile_buf, o_buf, z_buf, w_buf, w_now, x_sem, theta_sem, out_sem, init_sem, send_sem, recv_sem):
    me = lax.axis_index("seq")
    lag = me
    n_rows = n_batch * tok_dev
    n_steps = tok_dev // MINI_BATCH
    chunk = n_rows // n_steps
    depth = x_buf.shape[1]
    thetas = (theta_k_hbm, theta_v_hbm, theta_q_hbm)
    barrier = pltpu.get_barrier_semaphore()

    def columns(g):
        return pl.ds(pl.multiple_of(g * 256, 256), 256)

    def theta_copy(kind, g):
        return pltpu.make_async_copy(thetas[kind].at[:, columns(g)], theta_buf.at[lax.rem(3 * g + kind, 2)], theta_sem.at[lax.rem(3 * g + kind, 2)])

    def start_theta(tile):
        g = tile // 3
        for kind in range(3):
            @pl.when((lax.rem(tile, 3) == kind) & (tile < 3 * n_groups))
            def _():
                theta_copy(kind, g).start()

    def wait_theta(tile):
        slot = lax.rem(tile, 2)
        pltpu.make_async_copy(theta_k_hbm.at[:, pl.ds(0, 256)], theta_buf.at[slot], theta_sem.at[slot]).wait()

    def result(g):
        return pltpu.make_async_copy(o_buf, o_hbm.at[:, columns(g)], out_sem)

    def hand_on(g):
        return pltpu.make_async_remote_copy(w_buf.at[g], w_buf.at[g], send_sem.at[g], recv_sem.at[g],
                                            device_id={"seq": lax.rem(me + 1, n_seq)}, device_id_type=pl.DeviceIdType.MESH)

    def first_w(g, b):
        return pltpu.make_async_copy(w_init_hbm.at[g], w_buf.at[g, b], init_sem.at[g])

    def x_copy(i):
        rows = pl.ds(i * (n_rows // 2), n_rows // 2)
        return pltpu.make_async_copy(x_hbm.at[rows], x_buf.at[rows], x_sem.at[i])

    start_theta(jnp.int32(0))
    for i in range(2):
        x_copy(i).start()

    @pl.when(me == 0)
    def _():
        def body(g, _):
            for b in range(n_batch):
                first_w(g, b).start()
            return 0
        lax.fori_loop(0, n_groups, body, 0)

    for peer in (lax.rem(me + 1, n_seq), lax.rem(me + n_seq - 1, n_seq)):
        pl.semaphore_signal(barrier, inc=1, device_id={"seq": peer}, device_id_type=pl.DeviceIdType.MESH)
    pl.semaphore_wait(barrier, 2)
    for i in range(2):
        x_copy(i).wait()

    low = lax.broadcasted_iota(jnp.int32, (MINI_BATCH, 128), 1) < 64

    def whole_tile(tile):
        g, kind, slot = tile // 3, lax.rem(tile, 3), lax.rem(tile, 2)
        wait_theta(tile)
        start_theta(tile + 1)
        for i in range(2):
            rows = pl.ds(i * (n_rows // 2), n_rows // 2)
            kvq_buf[kind, g, rows, :] = jnp.dot(x_buf[rows, :], theta_buf[slot], preferred_element_type=f32).astype(bf16)

    def inner(g, tile):
        slot = lax.rem(tile, 2)

        @pl.when(tile < 3 * n_groups)
        def _():
            wait_theta(tile)
            start_theta(tile + 1)

        @pl.when(me == 0)
        def _():
            for b in range(n_batch):
                first_w(g, b).wait()

        @pl.when(me > 0)
        def _():
            hand_on(g).wait_recv()

        @pl.when(g > 0)
        def _():
            result(g - 1).wait()

        w_now[...] = w_buf[g]
        eta = eta_ref[g]

        def rows_of(b, j):
            start = b * tok_dev + j * MINI_BATCH
            return pl.ds(start if isinstance(start, int) else pl.multiple_of(start, MINI_BATCH), MINI_BATCH)

        half = n_batch // 2

        def multiply(b, j, with_k, with_q):
            rows = per_head_rows(kvq_buf[0, g, rows_of(b, j), :], low) if with_k else []
            if with_q:
                rows = rows + per_head_rows(kvq_buf[2, g, rows_of(b, j - 1), :], low)
            prod = times_w(rows, w_now[b])
            if with_k:
                z_buf[b] = own_columns(prod, low, 0)
            if with_q:
                o_buf[rows_of(b, j - 1), :] = own_columns(prod, low, 4 * MINI_BATCH if with_k else 0).astype(bf16)

        def update(b, j):
            r = (z_buf[b] - kvq_buf[1, g, rows_of(b, j), :].astype(f32)) * eta
            w_now[b] -= k_transposed_times(per_head_rows(kvq_buf[0, g, rows_of(b, j), :], low), r, low)

        def step(j, first=False):
            part = pl.ds(j * chunk if isinstance(j, int) else pl.multiple_of(j * chunk, chunk), chunk)
            tile_part = jnp.dot(x_buf[part, :], theta_buf[slot], preferred_element_type=f32)
            for b in range(half):
                multiply(b, j, True, not first)
                if not first:
                    update(half + b, j - 1)
            for b in range(half):
                multiply(half + b, j, True, not first)
                update(b, j)
            tile_buf[part, :] = tile_part.astype(bf16)

        step(0, True)

        def trip(i, _):
            for s in range(STEPS_PER_TRIP):
                step(1 + i * STEPS_PER_TRIP + s)
            return 0

        lax.fori_loop(0, (n_steps - 1) // STEPS_PER_TRIP, trip, 0)
        for b in range(half):
            update(half + b, n_steps - 1)

        @pl.when(me < n_seq - 1)
        def _():
            w_buf[g] = w_now[...]
            hand_on(g).start()

        for b in range(n_batch):
            multiply(b, n_steps, False, True)
        result(g).start()

        @pl.when(tile < 3 * n_groups)
        def _():
            kvq_buf[lax.rem(tile, 3), tile // 3] = tile_buf[...]

    def slot_body(s, _):
        g = s - 1 - lag

        @pl.when(g >= 0)
        def _():
            inner(g, 3 * s)

        def rest(kind, _):
            whole_tile(3 * s + kind)
            return 0

        @pl.when(s < n_groups)
        def _():
            lax.fori_loop(jnp.where(g >= 0, 1, 0), 3, rest, 0)
        return 0

    lax.fori_loop(0, n_groups + 1 + lag, slot_body, 0)

    result(n_groups - 1).wait()

    @pl.when(me < n_seq - 1)
    def _():
        for g in range(n_groups):
            hand_on(g).wait_send()


def solution(mesh):
    n_seq = mesh.shape["seq"]

    def per_device(tokens, theta_q, theta_k, theta_v, w_out, w_init, inner_lr):
        n_batch, tok_dev, width_d = tokens.shape
        n_heads, head_dim, _ = w_init.shape
        n_groups = n_heads // HEADS_PER_GROUP
        n_rows, width = n_batch * tok_dev, n_heads * head_dim
        flat = tokens.reshape(n_rows, width_d)
        w_start = w_init.reshape(n_groups, HEADS_PER_GROUP, head_dim, head_dim).transpose(0, 2, 1, 3).reshape(n_groups, head_dim, 4 * head_dim)
        eta = jnp.repeat((2.0 / MINI_BATCH) * inner_lr, head_dim).reshape(n_groups, 1, 4 * head_dim)
        hbm, vmem = pl.BlockSpec(memory_space=pl.ANY), pl.BlockSpec(memory_space=pltpu.VMEM)
        o = pl.pallas_call(
            functools.partial(fused_kernel, n_seq, n_batch, tok_dev, n_groups),
            out_shape=jax.ShapeDtypeStruct((n_rows, width), bf16),
            in_specs=[hbm] * 5 + [vmem], out_specs=hbm,
            scratch_shapes=[pltpu.VMEM((n_rows, width_d), bf16), pltpu.VMEM((3, n_groups, n_rows, 256), bf16),
                            pltpu.VMEM((2, width_d, 256), bf16), pltpu.VMEM((n_rows, 256), bf16), pltpu.VMEM((n_rows, 256), bf16), pltpu.VMEM((n_batch, MINI_BATCH, 256), f32),
                            pltpu.VMEM((n_groups, n_batch, head_dim, 4 * head_dim), f32),
                            pltpu.VMEM((n_batch, head_dim, 4 * head_dim), f32),
                            pltpu.SemaphoreType.DMA((2,)), pltpu.SemaphoreType.DMA((2,)), pltpu.SemaphoreType.DMA,
                            pltpu.SemaphoreType.DMA((n_groups,)), pltpu.SemaphoreType.DMA((n_groups,)), pltpu.SemaphoreType.DMA((n_groups,))],
            compiler_params=pltpu.CompilerParams(collective_id=0, has_side_effects=True, vmem_limit_bytes=67043328),
            name="fused",
        )(flat, theta_k, theta_v, theta_q, w_start, eta)
        result = jnp.dot(o, w_out, preferred_element_type=f32).astype(bf16)
        return result.reshape(n_batch, tok_dev, width_d)

    tok_spec = P("data", "seq", None)
    return jax.shard_map(per_device, mesh=mesh, in_specs=(tok_spec, P(), P(), P(), P(), P(), P()), out_specs=tok_spec, check_vma=False)
```

time: 368 us -> 322 us (0.88)
  matrix products: 187 us -> 46.9 us
  Pallas kernels: 177 us -> 270 us
    dot_general x3 -> x0, matrix products: 140 us -> none  [per_device(): jnp.dot(flat, theta, preferred_element_type=f32).astype(bf16)]
    pallas_call x1, Pallas kernels: 177 us -> 270 us  [per_device(): pl.pallas_call(functools.partial(fused_kernel, n_seq, n_batch, tok_dev, n...]
where the time goes in v3:
time: 322 us
  Pallas kernels  270 us (84%)
  matrix products  46.9 us (15%)
  local copies, waits for them, and re-layouts  5.04 us (2%)
    pallas_call x1, Pallas kernels, per_device(): pl.pallas_call(functools.partial(fused_kernel, n_seq, n_batch, tok_dev, n...  270 us
    dot_general x1, matrix products, per_device(): result = jnp.dot(o, w_out, preferred_element_type=f32).astype(bf16)  46.9 us

profile of v3, /device:TPU:127, one launch (start us, length us, event | category | flops | bytes accessed | tf_op | source)
XLA Modules:
  0.0 322.2 jit_solution(5411949955996904103)
XLA Ops:
  0.0 0.7 broadcast_multiply_fusion
  0.7 0.1 broadcast_in_dim.7
  0.7 0.1 broadcast_in_dim.8
  0.8 0.7 broadcast_in_dim.9.eta_ref
  1.5 2.4 copy.11
  4.0 1.8 reshape.21.w_init_hbm
  5.7 269.6 %fused.1 = bf16[2048,3072]{1,0:T(8,128)(2,1)} custom-call(bf16[2048,3072]{1,0:T(8,128)(2,1)} %bitcast.8, bf16[3072,3072]{1,0:T(8,128)(2,1)} %theta_k_hbm.1, bf16[3072,3072]{1,0:T(8,128)(2,1)} %theta_v_hbm.1, bf16[3072,3072]{1,0:T(8,128)(2,1)} %theta_q_hbm.1, f32[12,64,256]{2,1,0:T(8,128)} %reshape.21.w_init_hbm, f32[12,1,256]{2,1,0:T(1,128)} %broadcast_in_dim.9.eta_ref), custom_call_target="tpu_custom_call" | custom-call | tf_op jit(solution)/shard_map/fused/pallas_call | solution.py:248
  275.3 46.9 %convolution_convert_fusion = bf16[2048,3072]{1,0:T(8,128)(2,1)} fusion(bf16[2048,3072]{1,0:T(8,128)(2,1)} %fused.1, bf16[3072,3072]{1,0:T(8,128)(2,1)} %param.11), kind=kOutput, calls=%fused_computation | convolution fusion | flops 38660997120 | bytes 44040192 | tf_op jit(solution)/shard_map/dot_general | solution.py:261

commit v4 on v3

--- a/solution.py
+++ b/solution.py
@@ -10,6 +10,7 @@
 MINI_BATCH = 16
 HEADS_PER_GROUP = 4
 STEPS_PER_TRIP = 15
+SCHEDULE = ((0, 7), (1, 6), (2, 4), (3, 1), (3, 0), (3, 0), (5, 0), (7, 0))
 bf16, f32 = jnp.bfloat16, jnp.float32
 
 
@@ -58,9 +59,13 @@
 
 
 def fused_kernel(n_seq, n_batch, tok_dev, n_groups, x_hbm, theta_k_hbm, theta_v_hbm, theta_q_hbm, w_init_hbm, eta_ref, o_hbm,
-                 x_buf, kvq_buf, theta_buf, tile_buf, o_buf, z_buf, w_buf, w_now, x_sem, theta_sem, out_sem, init_sem, send_sem, recv_sem):
+                 x_buf, kvq_buf, theta_buf, tile_buf, o_buf, z_buf, w_buf, w_now, w_send, x_sem, theta_sem, out_sem, init_sem, send_sem, recv_sem):
     me = lax.axis_index("seq")
-    lag = me
+    lag, n_late = jnp.int32(0), jnp.int32(0)
+    for place, (ahead, late) in enumerate(SCHEDULE):
+        lag = jnp.where(me == place, ahead, lag)
+        n_late = jnp.where(me == place, late, n_late)
+    n_tiles = 3 * n_groups
     n_rows = n_batch * tok_dev
     n_steps = tok_dev // MINI_BATCH
     chunk = n_rows // n_steps
@@ -71,25 +76,28 @@
     def columns(g):
         return pl.ds(pl.multiple_of(g * 256, 256), 256)
 
-    def theta_copy(kind, g):
-        return pltpu.make_async_copy(thetas[kind].at[:, columns(g)], theta_buf.at[lax.rem(3 * g + kind, 2)], theta_sem.at[lax.rem(3 * g + kind, 2)])
-
-    def start_theta(tile):
-        g = tile // 3
-        for kind in range(3):
-            @pl.when((lax.rem(tile, 3) == kind) & (tile < 3 * n_groups))
+    def tile_at(c):
+        early, body = 2 * n_late, c - 2 * n_late
+        kind = jnp.where(c < early, lax.rem(c, 2), jnp.where(c < n_tiles - n_late, lax.rem(body, 3), 2))
+        g = jnp.where(c < early, c // 2, jnp.where(c < n_tiles - n_late, n_late + body // 3, c - (n_tiles - n_late)))
+        return kind, g
+
+    def start_theta(c):
+        kind, g = tile_at(c)
+        for i in range(3):
+            @pl.when((kind == i) & (c < n_tiles))
             def _():
-                theta_copy(kind, g).start()
-
-    def wait_theta(tile):
-        slot = lax.rem(tile, 2)
+                pltpu.make_async_copy(thetas[i].at[:, columns(g)], theta_buf.at[lax.rem(c, 2)], theta_sem.at[lax.rem(c, 2)]).start()
+
+    def wait_theta(c):
+        slot = lax.rem(c, 2)
         pltpu.make_async_copy(theta_k_hbm.at[:, pl.ds(0, 256)], theta_buf.at[slot], theta_sem.at[slot]).wait()
 
     def result(g):
         return pltpu.make_async_copy(o_buf, o_hbm.at[:, columns(g)], out_sem)
 
     def hand_on(g):
-        return pltpu.make_async_remote_copy(w_buf.at[g], w_buf.at[g], send_sem.at[g], recv_sem.at[g],
+        return pltpu.make_async_remote_copy(w_send, w_buf.at[g], send_sem, recv_sem.at[g],
                                             device_id={"seq": lax.rem(me + 1, n_seq)}, device_id_type=pl.DeviceIdType.MESH)
 
     def first_w(g, b):
@@ -119,34 +127,36 @@
 
     low = lax.broadcasted_iota(jnp.int32, (MINI_BATCH, 128), 1) < 64
 
-    def whole_tile(tile):
-        g, kind, slot = tile // 3, lax.rem(tile, 3), lax.rem(tile, 2)
-        wait_theta(tile)
-        start_theta(tile + 1)
+    def whole_tile(c):
+        kind, g = tile_at(c)
+        slot = lax.rem(c, 2)
+        wait_theta(c)
+        start_theta(c + 1)
         for i in range(2):
             rows = pl.ds(i * (n_rows // 2), n_rows // 2)
             kvq_buf[kind, g, rows, :] = jnp.dot(x_buf[rows, :], theta_buf[slot], preferred_element_type=f32).astype(bf16)
 
-    def inner(g, tile):
-        slot = lax.rem(tile, 2)
-
-        @pl.when(tile < 3 * n_groups)
-        def _():
-            wait_theta(tile)
-            start_theta(tile + 1)
-
-        @pl.when(me == 0)
+    def inner(g, first_time, c):
+        slot = lax.rem(c, 2)
+        has_q = jnp.logical_not(first_time) | (g >= n_late)
+
+        @pl.when(c < n_tiles)
+        def _():
+            wait_theta(c)
+            start_theta(c + 1)
+
+        @pl.when((me == 0) & first_time)
         def _():
             for b in range(n_batch):
                 first_w(g, b).wait()
 
-        @pl.when(me > 0)
+        @pl.when((me > 0) & first_time)
         def _():
             hand_on(g).wait_recv()
 
-        @pl.when(g > 0)
-        def _():
-            result(g - 1).wait()
+        @pl.when(has_q & jnp.where(first_time, g > n_late, (g > 0) | (n_late < n_groups)))
+        def _():
+            result(0).wait()
 
         w_now[...] = w_buf[g]
         eta = eta_ref[g]
@@ -194,43 +204,53 @@
         for b in range(half):
             update(half + b, n_steps - 1)
 
-        @pl.when(me < n_seq - 1)
-        def _():
-            w_buf[g] = w_now[...]
+        @pl.when((me < n_seq - 1) & first_time & (g > 0))
+        def _():
+            hand_on(0).wait_send()
+
+        @pl.when((me < n_seq - 1) & first_time)
+        def _():
+            w_send[...] = w_now[...]
             hand_on(g).start()
 
         for b in range(n_batch):
             multiply(b, n_steps, False, True)
-        result(g).start()
-
-        @pl.when(tile < 3 * n_groups)
-        def _():
-            kvq_buf[lax.rem(tile, 3), tile // 3] = tile_buf[...]
+
+        @pl.when(has_q)
+        def _():
+            result(g).start()
+
+        @pl.when(c < n_tiles)
+        def _():
+            kind, of = tile_at(c)
+            kvq_buf[kind, of] = tile_buf[...]
 
     def slot_body(s, _):
-        g = s - 1 - lag
+        first_time = s <= n_groups + lag
+        g = jnp.where(first_time, s - 1 - lag, s - (n_groups + 1 + lag))
+        fresh = s < n_groups
+        c = jnp.where(fresh, 2 * s + jnp.maximum(s - n_late, 0), n_tiles - n_late + s - n_groups)
 
         @pl.when(g >= 0)
         def _():
-            inner(g, 3 * s)
-
-        def rest(kind, _):
-            whole_tile(3 * s + kind)
+            inner(g, first_time, c)
+
+        def rest(i, _):
+            whole_tile(c + i)
             return 0
 
-        @pl.when(s < n_groups)
-        def _():
-            lax.fori_loop(jnp.where(g >= 0, 1, 0), 3, rest, 0)
+        @pl.when(fresh)
+        def _():
+            lax.fori_loop(jnp.where(g >= 0, 1, 0), jnp.where(s < n_late, 2, 3), rest, 0)
         return 0
 
-    lax.fori_loop(0, n_groups + 1 + lag, slot_body, 0)
-
-    result(n_groups - 1).wait()
+    lax.fori_loop(0, n_groups + 1 + lag + n_late, slot_body, 0)
+
+    result(0).wait()
 
     @pl.when(me < n_seq - 1)
     def _():
-        for g in range(n_groups):
-            hand_on(g).wait_send()
+        hand_on(0).wait_send()
 
 
 def solution(mesh):
@@ -252,9 +272,9 @@
             scratch_shapes=[pltpu.VMEM((n_rows, width_d), bf16), pltpu.VMEM((3, n_groups, n_rows, 256), bf16),
                             pltpu.VMEM((2, width_d, 256), bf16), pltpu.VMEM((n_rows, 256), bf16), pltpu.VMEM((n_rows, 256), bf16), pltpu.VMEM((n_batch, MINI_BATCH, 256), f32),
                             pltpu.VMEM((n_groups, n_batch, head_dim, 4 * head_dim), f32),
-                            pltpu.VMEM((n_batch, head_dim, 4 * head_dim), f32),
+                            pltpu.VMEM((n_batch, head_dim, 4 * head_dim), f32), pltpu.VMEM((n_batch, head_dim, 4 * head_dim), f32),
                             pltpu.SemaphoreType.DMA((2,)), pltpu.SemaphoreType.DMA((2,)), pltpu.SemaphoreType.DMA,
-                            pltpu.SemaphoreType.DMA((n_groups,)), pltpu.SemaphoreType.DMA((n_groups,)), pltpu.SemaphoreType.DMA((n_groups,))],
+                            pltpu.SemaphoreType.DMA((n_groups,)), pltpu.SemaphoreType.DMA, pltpu.SemaphoreType.DMA((n_groups,))],
             compiler_params=pltpu.CompilerParams(collective_id=0, has_side_effects=True, vmem_limit_bytes=67043328),
             name="fused",
         )(flat, theta_k, theta_v, theta_q, w_start, eta)

time: 322 us -> 304 us (0.944)
  Pallas kernels: 270 us -> 251 us
    pallas_call x1, Pallas kernels: 270 us -> 251 us  [per_device(): pl.pallas_call(functools.partial(fused_kernel, n_seq, n_batch, tok_dev, n...]
where the time goes in v4:
time: 304 us
  Pallas kernels  251 us (83%)
  matrix products  46.9 us (15%)
  local copies, waits for them, and re-layouts  5.04 us (2%)
    pallas_call x1, Pallas kernels, per_device(): pl.pallas_call(functools.partial(fused_kernel, n_seq, n_batch, tok_dev, n...  251 us
    dot_general x1, matrix products, per_device(): result = jnp.dot(o, w_out, preferred_element_type=f32).astype(bf16)  46.9 us

profile of v4, /device:TPU:127, one launch (start us, length us, event | category | flops | bytes accessed | tf_op | source)
XLA Modules:
  0.0 303.8 jit_solution(8300573111180566439)
XLA Ops:
  0.0 0.7 broadcast_multiply_fusion
  0.7 0.1 broadcast_in_dim.7
  0.7 0.1 broadcast_in_dim.8
  0.8 0.7 broadcast_in_dim.9.eta_ref
  1.5 2.4 copy.11
  4.0 1.8 reshape.21.w_init_hbm
  5.7 251.2 %fused.1 = bf16[2048,3072]{1,0:T(8,128)(2,1)} custom-call(bf16[2048,3072]{1,0:T(8,128)(2,1)} %bitcast.8, bf16[3072,3072]{1,0:T(8,128)(2,1)} %theta_k_hbm.1, bf16[3072,3072]{1,0:T(8,128)(2,1)} %theta_v_hbm.1, bf16[3072,3072]{1,0:T(8,128)(2,1)} %theta_q_hbm.1, f32[12,64,256]{2,1,0:T(8,128)} %reshape.21.w_init_hbm, f32[12,1,256]{2,1,0:T(1,128)} %broadcast_in_dim.9.eta_ref), custom_call_target="tpu_custom_call" | custom-call | tf_op jit(solution)/shard_map/fused/pallas_call | solution.py:268
  256.9 46.9 %convolution_convert_fusion = bf16[2048,3072]{1,0:T(8,128)(2,1)} fusion(bf16[2048,3072]{1,0:T(8,128)(2,1)} %fused.1, bf16[3072,3072]{1,0:T(8,128)(2,1)} %param.11), kind=kOutput, calls=%fused_computation | convolution fusion | flops 38660997120 | bytes 44040192 | tf_op jit(solution)/shard_map/dot_general | solution.py:281

commit v5 on v4

--- a/solution.py
+++ b/solution.py
@@ -10,7 +10,8 @@
 MINI_BATCH = 16
 HEADS_PER_GROUP = 4
 STEPS_PER_TRIP = 15
-SCHEDULE = ((0, 7), (1, 6), (2, 4), (3, 1), (3, 0), (3, 0), (5, 0), (7, 0))
+SCHEDULE = ((0, 7, 0), (1, 6, 0), (2, 4, 0), (3, 1, 0), (3, 0, 1), (3, 0, 1), (5, 0, 1), (7, 0, 1))
+N_FIRST = 8
 bf16, f32 = jnp.bfloat16, jnp.float32
 
 
@@ -58,14 +59,18 @@
     return jnp.dot(lhs, rhs, preferred_element_type=f32)
 
 
-def fused_kernel(n_seq, n_batch, tok_dev, n_groups, x_hbm, theta_k_hbm, theta_v_hbm, theta_q_hbm, w_init_hbm, eta_ref, o_hbm,
-                 x_buf, kvq_buf, theta_buf, tile_buf, o_buf, z_buf, w_buf, w_now, w_send, x_sem, theta_sem, out_sem, init_sem, send_sem, recv_sem):
+def fused_kernel(n_seq, n_batch, tok_dev, n_groups, x_hbm, theta_k_hbm, theta_v_hbm, theta_q_hbm, w_out_hbm, w_init_hbm, eta_ref, o_hbm, sum_hbm,
+                 x_buf, kvq_buf, theta_buf, tile_buf, o_buf, z_buf, w_buf, w_now, w_send, init_buf, x_sem, theta_sem, out_sem, sum_sem, init_sem, send_sem, recv_sem):
     me = lax.axis_index("seq")
-    lag, n_late = jnp.int32(0), jnp.int32(0)
-    for place, (ahead, late) in enumerate(SCHEDULE):
+    lag, n_late, early_out = jnp.int32(0), jnp.int32(0), jnp.int32(0)
+    for place, (ahead, late, early) in enumerate(SCHEDULE):
         lag = jnp.where(me == place, ahead, lag)
         n_late = jnp.where(me == place, late, n_late)
+        early_out = jnp.where(me == place, early, early_out)
     n_tiles = 3 * n_groups
+    n_out_tiles = sum_hbm.shape[-1] // 256
+    first_depth = N_FIRST * 256
+    outs_per_slot = n_out_tiles // (n_groups - N_FIRST)
     n_rows = n_batch * tok_dev
     n_steps = tok_dev // MINI_BATCH
     chunk = n_rows // n_steps
@@ -89,19 +94,32 @@
             def _():
                 pltpu.make_async_copy(thetas[i].at[:, columns(g)], theta_buf.at[lax.rem(c, 2)], theta_sem.at[lax.rem(c, 2)]).start()
 
+        @pl.when((c >= n_tiles) & (c < n_tiles + n_out_tiles))
+        def _():
+            w_out_copy(c - n_tiles, lax.rem(c, 2)).start()
+
+    def w_out_copy(n, slot):
+        return pltpu.make_async_copy(w_out_hbm.at[pl.ds(0, first_depth), columns(n)], theta_buf.at[slot, pl.ds(0, first_depth)], theta_sem.at[slot])
+
     def wait_theta(c):
         slot = lax.rem(c, 2)
         pltpu.make_async_copy(theta_k_hbm.at[:, pl.ds(0, 256)], theta_buf.at[slot], theta_sem.at[slot]).wait()
 
     def result(g):
-        return pltpu.make_async_copy(o_buf, o_hbm.at[:, columns(g)], out_sem)
+        return pltpu.make_async_copy(o_buf, o_hbm.at[:, columns(g - N_FIRST)], out_sem)
+
+    def sum_copy(n):
+        part = lax.rem(n, 2)
+        return pltpu.make_async_copy(w_buf.at[pl.ds(part * sum_slots, sum_slots)], sum_hbm.at[:, :, :, columns(n)], sum_sem.at[part])
 
     def hand_on(g):
         return pltpu.make_async_remote_copy(w_send, w_buf.at[g], send_sem, recv_sem.at[g],
                                             device_id={"seq": lax.rem(me + 1, n_seq)}, device_id_type=pl.DeviceIdType.MESH)
 
-    def first_w(g, b):
-        return pltpu.make_async_copy(w_init_hbm.at[g], w_buf.at[g, b], init_sem.at[g])
+    sum_slots = sum_hbm.shape[0]
+
+    def first_w(g):
+        return pltpu.make_async_copy(w_init_hbm.at[pl.ds(g * HEADS_PER_GROUP, HEADS_PER_GROUP)], init_buf, init_sem)
 
     def x_copy(i):
         rows = pl.ds(i * (n_rows // 2), n_rows // 2)
@@ -113,11 +131,7 @@
 
     @pl.when(me == 0)
     def _():
-        def body(g, _):
-            for b in range(n_batch):
-                first_w(g, b).start()
-            return 0
-        lax.fori_loop(0, n_groups, body, 0)
+        first_w(0).start()
 
     for peer in (lax.rem(me + 1, n_seq), lax.rem(me + n_seq - 1, n_seq)):
         pl.semaphore_signal(barrier, inc=1, device_id={"seq": peer}, device_id_type=pl.DeviceIdType.MESH)
@@ -136,8 +150,25 @@
             rows = pl.ds(i * (n_rows // 2), n_rows // 2)
             kvq_buf[kind, g, rows, :] = jnp.dot(x_buf[rows, :], theta_buf[slot], preferred_element_type=f32).astype(bf16)
 
+    def out_tile(n):
+        c = n_tiles + n
+        slot = lax.rem(c, 2)
+        w_out_copy(n, slot).wait()
+        start_theta(c + 1)
+
+        @pl.when(n >= 2)
+        def _():
+            sum_copy(n - 2).wait()
+
+        for i in range(2):
+            rows = pl.ds(i * (n_rows // 2), n_rows // 2)
+            lhs = jnp.concatenate([kvq_buf[2, g, rows, :] for g in range(N_FIRST)], axis=1)
+            part = jnp.dot(lhs, theta_buf[slot, :first_depth, :], preferred_element_type=f32)
+            w_buf[pl.ds(lax.rem(n, 2) * sum_slots + i * (sum_slots // 2), sum_slots // 2)] = part.reshape(sum_slots // 2, *w_buf.shape[1:])
+        sum_copy(n).start()
+
     def inner(g, first_time, c):
-        slot = lax.rem(c, 2)
+        slot = lax.rem(jnp.where(c < n_tiles, c, c - 1), 2)
         has_q = jnp.logical_not(first_time) | (g >= n_late)
 
         @pl.when(c < n_tiles)
@@ -147,16 +178,22 @@
 
         @pl.when((me == 0) & first_time)
         def _():
+            first_w(g).wait()
+            start = jnp.concatenate([init_buf[h] for h in range(HEADS_PER_GROUP)], axis=1)
             for b in range(n_batch):
-                first_w(g, b).wait()
+                w_buf[g, b] = start
+
+        @pl.when((me == 0) & first_time & (g + 1 < n_groups))
+        def _():
+            first_w(g + 1).start()
 
         @pl.when((me > 0) & first_time)
         def _():
             hand_on(g).wait_recv()
 
-        @pl.when(has_q & jnp.where(first_time, g > n_late, (g > 0) | (n_late < n_groups)))
-        def _():
-            result(0).wait()
+        @pl.when(jnp.where(first_time, g > N_FIRST, g == 0))
+        def _():
+            result(N_FIRST).wait()
 
         w_now[...] = w_buf[g]
         eta = eta_ref[g]
@@ -216,9 +253,13 @@
         for b in range(n_batch):
             multiply(b, n_steps, False, True)
 
-        @pl.when(has_q)
+        @pl.when(has_q & (g >= N_FIRST))
         def _():
             result(g).start()
+
+        @pl.when(has_q & (g < N_FIRST))
+        def _():
+            kvq_buf[2, g] = o_buf[...]
 
         @pl.when(c < n_tiles)
         def _():
@@ -229,11 +270,20 @@
         first_time = s <= n_groups + lag
         g = jnp.where(first_time, s - 1 - lag, s - (n_groups + 1 + lag))
         fresh = s < n_groups
-        c = jnp.where(fresh, 2 * s + jnp.maximum(s - n_late, 0), n_tiles - n_late + s - n_groups)
+        c = jnp.where(fresh, 2 * s + jnp.maximum(s - n_late, 0), jnp.minimum(n_tiles - n_late + s - n_groups, n_tiles))
+        out_now = (early_out > 0) & first_time & (g >= N_FIRST)
+        n_out = jnp.where(out_now, outs_per_slot * (g - N_FIRST), 0)
+
+        def outs(n, _):
+            out_tile(n)
+            return 0
+
+        lax.fori_loop(n_out, jnp.where(out_now, n_out + outs_per_slot, n_out), outs, 0)
+        c_inner = jnp.where(out_now, n_tiles + n_out + outs_per_slot, c)
 
         @pl.when(g >= 0)
         def _():
-            inner(g, first_time, c)
+            inner(g, first_time, c_inner)
 
         def rest(i, _):
             whole_tile(c + i)
@@ -246,7 +296,17 @@
 
     lax.fori_loop(0, n_groups + 1 + lag + n_late, slot_body, 0)
 
-    result(0).wait()
+    def outs(n, _):
+        out_tile(n)
+        return 0
+
+    lax.fori_loop(jnp.where(early_out > 0, n_out_tiles, 0), n_out_tiles, outs, 0)
+    for n in range(2):
+        sum_copy(n_out_tiles - 2 + n).wait()
+
+    @pl.when(n_late == 0)
+    def _():
+        result(N_FIRST).wait()
 
     @pl.when(me < n_seq - 1)
     def _():
@@ -262,23 +322,25 @@
         n_groups = n_heads // HEADS_PER_GROUP
         n_rows, width = n_batch * tok_dev, n_heads * head_dim
         flat = tokens.reshape(n_rows, width_d)
-        w_start = w_init.reshape(n_groups, HEADS_PER_GROUP, head_dim, head_dim).transpose(0, 2, 1, 3).reshape(n_groups, head_dim, 4 * head_dim)
         eta = jnp.repeat((2.0 / MINI_BATCH) * inner_lr, head_dim).reshape(n_groups, 1, 4 * head_dim)
         hbm, vmem = pl.BlockSpec(memory_space=pl.ANY), pl.BlockSpec(memory_space=pltpu.VMEM)
-        o = pl.pallas_call(
+        sum_slots = n_rows // (n_batch * head_dim)
+        o, first_sum = pl.pallas_call(
             functools.partial(fused_kernel, n_seq, n_batch, tok_dev, n_groups),
-            out_shape=jax.ShapeDtypeStruct((n_rows, width), bf16),
-            in_specs=[hbm] * 5 + [vmem], out_specs=hbm,
+            out_shape=(jax.ShapeDtypeStruct((n_rows, width - 256 * N_FIRST), bf16), jax.ShapeDtypeStruct((sum_slots, n_batch, head_dim, width_d), f32)),
+            in_specs=[hbm] * 6 + [vmem], out_specs=(hbm, hbm),
             scratch_shapes=[pltpu.VMEM((n_rows, width_d), bf16), pltpu.VMEM((3, n_groups, n_rows, 256), bf16),
                             pltpu.VMEM((2, width_d, 256), bf16), pltpu.VMEM((n_rows, 256), bf16), pltpu.VMEM((n_rows, 256), bf16), pltpu.VMEM((n_batch, MINI_BATCH, 256), f32),
                             pltpu.VMEM((n_groups, n_batch, head_dim, 4 * head_dim), f32),
                             pltpu.VMEM((n_batch, head_dim, 4 * head_dim), f32), pltpu.VMEM((n_batch, head_dim, 4 * head_dim), f32),
-                            pltpu.SemaphoreType.DMA((2,)), pltpu.SemaphoreType.DMA((2,)), pltpu.SemaphoreType.DMA,
-                            pltpu.SemaphoreType.DMA((n_groups,)), pltpu.SemaphoreType.DMA, pltpu.SemaphoreType.DMA((n_groups,))],
+                            pltpu.VMEM((HEADS_PER_GROUP, head_dim, head_dim), f32),
+                            pltpu.SemaphoreType.DMA((2,)), pltpu.SemaphoreType.DMA((2,)), pltpu.SemaphoreType.DMA, pltpu.SemaphoreType.DMA((2,)),
+                            pltpu.SemaphoreType.DMA, pltpu.SemaphoreType.DMA, pltpu.SemaphoreType.DMA((n_groups,))],
             compiler_params=pltpu.CompilerParams(collective_id=0, has_side_effects=True, vmem_limit_bytes=67043328),
             name="fused",
-        )(flat, theta_k, theta_v, theta_q, w_start, eta)
-        result = jnp.dot(o, w_out, preferred_element_type=f32).astype(bf16)
+        )(flat, theta_k, theta_v, theta_q, w_out, w_init, eta)
+        rest = jnp.dot(o, w_out[256 * N_FIRST:], preferred_element_type=f32)
+        result = (rest + first_sum.reshape(n_rows, width_d)).astype(bf16)
         return result.reshape(n_batch, tok_dev, width_d)
 
     tok_spec = P("data", "seq", None)

time: 304 us -> 298 us (0.980)
  matrix products: 46.9 us -> 21.9 us
  Pallas kernels: 251 us -> 275 us
  local copies, waits for them, and re-layouts: 5.04 us -> 0.86 us
    dot_general x1, matrix products: 46.9 us -> 21.9 us  [per_device(): rest = jnp.dot(o, w_out[256 * N_FIRST:], preferred_element_type=f32)]
    pallas_call x1, Pallas kernels: 251 us -> 275 us  [per_device(): pl.pallas_call(functools.partial(fused_kernel, n_seq, n_batch, tok_dev, n...]
    reshape x2 -> x0, local copies, waits for them, and re-layouts: 4.18 us -> none  [per_device(): w_init.reshape(n_groups, HEADS_PER_GROUP, head_dim, head_dim)]
where the time goes in v5:
time: 298 us
  Pallas kernels  275 us (92%)
  matrix products  21.9 us (7%)
    pallas_call x1, Pallas kernels, per_device(): pl.pallas_call(functools.partial(fused_kernel, n_seq, n_batch, tok_dev, n...  275 us
    dot_general x1, matrix products, per_device(): rest = jnp.dot(o, w_out[256 * N_FIRST:], preferred_element_type=f32)  21.9 us

profile of v5, /device:TPU:127, one launch (start us, length us, event | category | flops | bytes accessed | tf_op | source)
XLA Modules:
  0.0 298.0 jit_solution(18426567679756089547)
XLA Ops:
  0.0 0.7 broadcast_multiply_fusion
  0.7 0.1 broadcast_in_dim.7
  0.7 0.1 broadcast_in_dim.8
  0.8 0.7 broadcast_in_dim.9.eta_ref
  1.5 274.6 %fused.1 = (bf16[2048,1024]{1,0:T(8,128)(2,1)}, f32[4,8,64,3072]{3,2,1,0:T(8,128)}) custom-call(bf16[2048,3072]{1,0:T(8,128)(2,1)} %bitcast.7, bf16[3072,3072]{1,0:T(8,128)(2,1)} %theta_k_hbm.1, bf16[3072,3072]{1,0:T(8,128)(2,1)} %theta_v_hbm.1, bf16[3072,3072]{1,0:T(8,128)(2,1)} %theta_q_hbm.1, bf16[3072,3072]{1,0:T(8,128)(2,1)} %w_out_hbm.1, ...), custom_call_target="tpu_custom_call" | custom-call | tf_op jit(solution)/shard_map/fused/pallas_call | solution.py:328
  276.1 21.9 %fusion = bf16[2048,3072]{1,0:T(8,128)(2,1)} fusion(f32[4,8,64,3072]{3,2,1,0:T(8,128)} %get-tuple-element.8, bf16[2048,1024]{1,0:T(8,128)(2,1)} %get-tuple-element.7, bf16[3072,3072]{1,0:T(8,128)(2,1)} %w_out_hbm.1), kind=kOutput, calls=%fused_computation.1 | convolution fusion | flops 12897484800 | bytes 48234496 | tf_op jit(solution)/shard_map/dot_general | solution.py:342

commit v6 on v5

--- a/solution.py
+++ b/solution.py
@@ -9,9 +9,10 @@
 
 MINI_BATCH = 16
 HEADS_PER_GROUP = 4
-STEPS_PER_TRIP = 15
-SCHEDULE = ((0, 7, 0), (1, 6, 0), (2, 4, 0), (3, 1, 0), (3, 0, 1), (3, 0, 1), (5, 0, 1), (7, 0, 1))
+SCHEDULE = ((0, 3, (0, 0, 0, 0)), (1, 2, (0, 0, 0, 0)), (1, 1, (0, 0, 0, 0)), (2, 1, (0, 0, 0, 0)),
+            (4, 0, (4, 7, 10, 10)), (5, 0, (6, 10, 10, 10)), (7, 0, (11, 11, 11, 11)), (8, 0, (11, 11, 11, 11)))
 N_FIRST = 8
+FILL = 768
 bf16, f32 = jnp.bfloat16, jnp.float32
 
 
@@ -62,15 +63,21 @@
 def fused_kernel(n_seq, n_batch, tok_dev, n_groups, x_hbm, theta_k_hbm, theta_v_hbm, theta_q_hbm, w_out_hbm, w_init_hbm, eta_ref, o_hbm, sum_hbm,
                  x_buf, kvq_buf, theta_buf, tile_buf, o_buf, z_buf, w_buf, w_now, w_send, init_buf, x_sem, theta_sem, out_sem, sum_sem, init_sem, send_sem, recv_sem):
     me = lax.axis_index("seq")
-    lag, n_late, early_out = jnp.int32(0), jnp.int32(0), jnp.int32(0)
-    for place, (ahead, late, early) in enumerate(SCHEDULE):
+    lag, n_late = jnp.int32(0), jnp.int32(0)
+    for place, (ahead, late, _) in enumerate(SCHEDULE):
         lag = jnp.where(me == place, ahead, lag)
         n_late = jnp.where(me == place, late, n_late)
-        early_out = jnp.where(me == place, early, early_out)
+
+    def outs_before(g):
+        n = jnp.int32(0)
+        for place, (_, _, counts) in enumerate(SCHEDULE):
+            for i, count in enumerate(counts):
+                n = jnp.where((me == place) & (g >= N_FIRST + i), count, n)
+        return n
+
     n_tiles = 3 * n_groups
     n_out_tiles = sum_hbm.shape[-1] // 256
     first_depth = N_FIRST * 256
-    outs_per_slot = n_out_tiles // (n_groups - N_FIRST)
     n_rows = n_batch * tok_dev
     n_steps = tok_dev // MINI_BATCH
     chunk = n_rows // n_steps
@@ -167,7 +174,7 @@
             w_buf[pl.ds(lax.rem(n, 2) * sum_slots + i * (sum_slots // 2), sum_slots // 2)] = part.reshape(sum_slots // 2, *w_buf.shape[1:])
         sum_copy(n).start()
 
-    def inner(g, first_time, c):
+    def inner(g, first_time, c, fill):
         slot = lax.rem(jnp.where(c < n_tiles, c, c - 1), 2)
         has_q = jnp.logical_not(first_time) | (g >= n_late)
 
@@ -195,7 +202,6 @@
         def _():
             result(N_FIRST).wait()
 
-        w_now[...] = w_buf[g]
         eta = eta_ref[g]
 
         def rows_of(b, j):
@@ -208,36 +214,36 @@
             rows = per_head_rows(kvq_buf[0, g, rows_of(b, j), :], low) if with_k else []
             if with_q:
                 rows = rows + per_head_rows(kvq_buf[2, g, rows_of(b, j - 1), :], low)
-            prod = times_w(rows, w_now[b])
+            prod = times_w(rows, w_now[b] if with_k and with_q or not with_k else w_buf[g, b])
             if with_k:
                 z_buf[b] = own_columns(prod, low, 0)
             if with_q:
                 o_buf[rows_of(b, j - 1), :] = own_columns(prod, low, 4 * MINI_BATCH if with_k else 0).astype(bf16)
 
-        def update(b, j):
+        def update(b, j, first=False):
             r = (z_buf[b] - kvq_buf[1, g, rows_of(b, j), :].astype(f32)) * eta
-            w_now[b] -= k_transposed_times(per_head_rows(kvq_buf[0, g, rows_of(b, j), :], low), r, low)
-
-        def step(j, first=False):
+            w_now[b] = (w_buf[g, b] if first else w_now[b]) - k_transposed_times(per_head_rows(kvq_buf[0, g, rows_of(b, j), :], low), r, low)
+
+        def step(j, first=False, second=False):
             part = pl.ds(j * chunk if isinstance(j, int) else pl.multiple_of(j * chunk, chunk), chunk)
-            tile_part = jnp.dot(x_buf[part, :], theta_buf[slot], preferred_element_type=f32)
+            tile_part = jnp.dot(x_buf[part, :fill], theta_buf[slot, :fill, :], preferred_element_type=f32)
             for b in range(half):
                 multiply(b, j, True, not first)
                 if not first:
-                    update(half + b, j - 1)
+                    update(half + b, j - 1, second)
             for b in range(half):
                 multiply(half + b, j, True, not first)
-                update(b, j)
+                update(b, j, first)
             tile_buf[part, :] = tile_part.astype(bf16)
 
-        step(0, True)
-
-        def trip(i, _):
-            for s in range(STEPS_PER_TRIP):
-                step(1 + i * STEPS_PER_TRIP + s)
+        step(0, first=True)
+        step(1, second=True)
+
+        def later_step(j, _):
+            step(j)
             return 0
 
-        lax.fori_loop(0, (n_steps - 1) // STEPS_PER_TRIP, trip, 0)
+        lax.fori_loop(2, n_steps, later_step, 0)
         for b in range(half):
             update(half + b, n_steps - 1)
 
@@ -271,19 +277,21 @@
         g = jnp.where(first_time, s - 1 - lag, s - (n_groups + 1 + lag))
         fresh = s < n_groups
         c = jnp.where(fresh, 2 * s + jnp.maximum(s - n_late, 0), jnp.minimum(n_tiles - n_late + s - n_groups, n_tiles))
-        out_now = (early_out > 0) & first_time & (g >= N_FIRST)
-        n_out = jnp.where(out_now, outs_per_slot * (g - N_FIRST), 0)
+        n_out = jnp.where(first_time, outs_before(g), 0)
 
         def outs(n, _):
             out_tile(n)
             return 0
 
-        lax.fori_loop(n_out, jnp.where(out_now, n_out + outs_per_slot, n_out), outs, 0)
-        c_inner = jnp.where(out_now, n_tiles + n_out + outs_per_slot, c)
-
-        @pl.when(g >= 0)
-        def _():
-            inner(g, first_time, c_inner)
+        lax.fori_loop(jnp.where(first_time, outs_before(g - 1), 0), n_out, outs, 0)
+
+        @pl.when((g >= 0) & (c < n_tiles))
+        def _():
+            inner(g, first_time, c + n_out, depth)
+
+        @pl.when((g >= 0) & (c >= n_tiles))
+        def _():
+            inner(g, first_time, c + n_out, FILL)
 
         def rest(i, _):
             whole_tile(c + i)
@@ -300,7 +308,7 @@
         out_tile(n)
         return 0
 
-    lax.fori_loop(jnp.where(early_out > 0, n_out_tiles, 0), n_out_tiles, outs, 0)
+    lax.fori_loop(outs_before(n_groups), n_out_tiles, outs, 0)
     for n in range(2):
         sum_copy(n_out_tiles - 2 + n).wait()
 

time: 298 us -> 347 us (1.16)
  Pallas kernels: 275 us -> 323 us
    pallas_call x1, Pallas kernels: 275 us -> 323 us  [per_device(): pl.pallas_call(functools.partial(fused_kernel, n_seq, n_batch, tok_dev, n...]
where the time goes in v6:
time: 347 us
  Pallas kernels  323 us (93%)
  matrix products  22.1 us (6%)
    pallas_call x1, Pallas kernels, per_device(): pl.pallas_call(functools.partial(fused_kernel, n_seq, n_batch, tok_dev, n...  323 us
    dot_general x1, matrix products, per_device(): rest = jnp.dot(o, w_out[256 * N_FIRST:], preferred_element_type=f32)  22.1 us

profile of v6, /device:TPU:127, one launch (start us, length us, event | category | flops | bytes accessed | tf_op | source)
XLA Modules:
  0.0 346.9 jit_solution(2021193466769466786)
XLA Ops:
  0.0 0.7 broadcast_multiply_fusion
  0.7 0.1 broadcast_in_dim.7
  0.7 0.1 broadcast_in_dim.8
  0.8 0.7 broadcast_in_dim.9.eta_ref
  1.5 323.3 %fused.1 = (bf16[2048,1024]{1,0:T(8,128)(2,1)}, f32[4,8,64,3072]{3,2,1,0:T(8,128)}) custom-call(bf16[2048,3072]{1,0:T(8,128)(2,1)} %bitcast.7, bf16[3072,3072]{1,0:T(8,128)(2,1)} %theta_k_hbm.1, bf16[3072,3072]{1,0:T(8,128)(2,1)} %theta_v_hbm.1, bf16[3072,3072]{1,0:T(8,128)(2,1)} %theta_q_hbm.1, bf16[3072,3072]{1,0:T(8,128)(2,1)} %w_out_hbm.1, ...), custom_call_target="tpu_custom_call" | custom-call | tf_op jit(solution)/shard_map/fused/pallas_call | solution.py:336
  324.9 22.1 %fusion = bf16[2048,3072]{1,0:T(8,128)(2,1)} fusion(f32[4,8,64,3072]{3,2,1,0:T(8,128)} %get-tuple-element.8, bf16[2048,1024]{1,0:T(8,128)(2,1)} %get-tuple-element.7, bf16[3072,3072]{1,0:T(8,128)(2,1)} %w_out_hbm.1), kind=kOutput, calls=%fused_computation.1 | convolution fusion | flops 12897484800 | bytes 48234496 | tf_op jit(solution)/shard_map/dot_general | solution.py:350

commit v7 on v6

--- a/solution.py
+++ b/solution.py
@@ -174,7 +174,7 @@
             w_buf[pl.ds(lax.rem(n, 2) * sum_slots + i * (sum_slots // 2), sum_slots // 2)] = part.reshape(sum_slots // 2, *w_buf.shape[1:])
         sum_copy(n).start()
 
-    def inner(g, first_time, c, fill):
+    def inner(g, first_time, c, fill, per_trip):
         slot = lax.rem(jnp.where(c < n_tiles, c, c - 1), 2)
         has_q = jnp.logical_not(first_time) | (g >= n_late)
 
@@ -211,7 +211,7 @@
         half = n_batch // 2
 
         def multiply(b, j, with_k, with_q):
-            rows = per_head_rows(kvq_buf[0, g, rows_of(b, j), :], low) if with_k else []
+            k_rows = rows = per_head_rows(kvq_buf[0, g, rows_of(b, j), :], low) if with_k else []
             if with_q:
                 rows = rows + per_head_rows(kvq_buf[2, g, rows_of(b, j - 1), :], low)
             prod = times_w(rows, w_now[b] if with_k and with_q or not with_k else w_buf[g, b])
@@ -219,31 +219,35 @@
                 z_buf[b] = own_columns(prod, low, 0)
             if with_q:
                 o_buf[rows_of(b, j - 1), :] = own_columns(prod, low, 4 * MINI_BATCH if with_k else 0).astype(bf16)
-
-        def update(b, j, first=False):
+            return k_rows
+
+        def update(b, j, k_rows=None, first=False):
+            k_rows = k_rows or per_head_rows(kvq_buf[0, g, rows_of(b, j), :], low)
             r = (z_buf[b] - kvq_buf[1, g, rows_of(b, j), :].astype(f32)) * eta
-            w_now[b] = (w_buf[g, b] if first else w_now[b]) - k_transposed_times(per_head_rows(kvq_buf[0, g, rows_of(b, j), :], low), r, low)
+            w_now[b] = (w_buf[g, b] if first else w_now[b]) - k_transposed_times(k_rows, r, low)
 
         def step(j, first=False, second=False):
             part = pl.ds(j * chunk if isinstance(j, int) else pl.multiple_of(j * chunk, chunk), chunk)
             tile_part = jnp.dot(x_buf[part, :fill], theta_buf[slot, :fill, :], preferred_element_type=f32)
+            k_rows = {}
             for b in range(half):
-                multiply(b, j, True, not first)
+                k_rows[b] = multiply(b, j, True, not first)
                 if not first:
-                    update(half + b, j - 1, second)
+                    update(half + b, j - 1, first=second)
             for b in range(half):
                 multiply(half + b, j, True, not first)
-                update(b, j, first)
+                update(b, j, k_rows[b], first)
             tile_buf[part, :] = tile_part.astype(bf16)
 
         step(0, first=True)
         step(1, second=True)
 
-        def later_step(j, _):
-            step(j)
+        def later_steps(i, _):
+            for s in range(per_trip):
+                step(2 + i * per_trip + s)
             return 0
 
-        lax.fori_loop(2, n_steps, later_step, 0)
+        lax.fori_loop(0, (n_steps - 2) // per_trip, later_steps, 0)
         for b in range(half):
             update(half + b, n_steps - 1)
 
@@ -287,11 +291,11 @@
 
         @pl.when((g >= 0) & (c < n_tiles))
         def _():
-            inner(g, first_time, c + n_out, depth)
+            inner(g, first_time, c + n_out, depth, (n_steps - 2) // 2)
 
         @pl.when((g >= 0) & (c >= n_tiles))
         def _():
-            inner(g, first_time, c + n_out, FILL)
+            inner(g, first_time, c + n_out, FILL, (n_steps - 2) // 2)
 
         def rest(i, _):
             whole_tile(c + i)

time: 347 us -> 296 us (0.85)
  Pallas kernels: 323 us -> 272 us
    pallas_call x1, Pallas kernels: 323 us -> 272 us  [per_device(): pl.pallas_call(functools.partial(fused_kernel, n_seq, n_batch, tok_dev, n...]
where the time goes in v7:
time: 296 us
  Pallas kernels  272 us (92%)
  matrix products  21.9 us (7%)
    pallas_call x1, Pallas kernels, per_device(): pl.pallas_call(functools.partial(fused_kernel, n_seq, n_batch, tok_dev, n...  272 us
    dot_general x1, matrix products, per_device(): rest = jnp.dot(o, w_out[256 * N_FIRST:], preferred_element_type=f32)  21.9 us

profile of v7, /device:TPU:127, one launch (start us, length us, event | category | flops | bytes accessed | tf_op | source)
XLA Modules:
  0.0 295.5 jit_solution(5381251908533699705)
XLA Ops:
  0.0 0.7 broadcast_multiply_fusion
  0.7 0.1 broadcast_in_dim.7
  0.7 0.1 broadcast_in_dim.8
  0.8 0.7 broadcast_in_dim.9.eta_ref
  1.5 272.1 %fused.1 = (bf16[2048,1024]{1,0:T(8,128)(2,1)}, f32[4,8,64,3072]{3,2,1,0:T(8,128)}) custom-call(bf16[2048,3072]{1,0:T(8,128)(2,1)} %bitcast.7, bf16[3072,3072]{1,0:T(8,128)(2,1)} %theta_k_hbm.1, bf16[3072,3072]{1,0:T(8,128)(2,1)} %theta_v_hbm.1, bf16[3072,3072]{1,0:T(8,128)(2,1)} %theta_q_hbm.1, bf16[3072,3072]{1,0:T(8,128)(2,1)} %w_out_hbm.1, ...), custom_call_target="tpu_custom_call" | custom-call | tf_op jit(solution)/shard_map/fused/pallas_call | solution.py:340
  273.6 21.9 %fusion = bf16[2048,3072]{1,0:T(8,128)(2,1)} fusion(f32[4,8,64,3072]{3,2,1,0:T(8,128)} %get-tuple-element.8, bf16[2048,1024]{1,0:T(8,128)(2,1)} %get-tuple-element.7, bf16[3072,3072]{1,0:T(8,128)(2,1)} %w_out_hbm.1), kind=kOutput, calls=%fused_computation.1 | convolution fusion | flops 12897484800 | bytes 48234496 | tf_op jit(solution)/shard_map/dot_general | solution.py:354

commit v8 on v7

--- a/solution.py
+++ b/solution.py
@@ -9,10 +9,10 @@
 
 MINI_BATCH = 16
 HEADS_PER_GROUP = 4
-SCHEDULE = ((0, 3, (0, 0, 0, 0)), (1, 2, (0, 0, 0, 0)), (1, 1, (0, 0, 0, 0)), (2, 1, (0, 0, 0, 0)),
-            (4, 0, (4, 7, 10, 10)), (5, 0, (6, 10, 10, 10)), (7, 0, (11, 11, 11, 11)), (8, 0, (11, 11, 11, 11)))
+SCHEDULE = ((0, 6, (0, 0, 0, 0)), (1, 5, (0, 0, 0, 0)), (2, 4, (0, 0, 0, 0)), (2, 4, (0, 0, 0, 0)),
+            (5, 2, (0, 0, 0, 0)), (5, 0, (4, 8, 8, 9)), (7, 0, (8, 8, 11, 11)), (7, 0, (10, 11, 11, 11)))
 N_FIRST = 8
-FILL = 768
+REST_COLUMNS = 512
 bf16, f32 = jnp.bfloat16, jnp.float32
 
 
@@ -142,20 +142,39 @@
 
     for peer in (lax.rem(me + 1, n_seq), lax.rem(me + n_seq - 1, n_seq)):
         pl.semaphore_signal(barrier, inc=1, device_id={"seq": peer}, device_id_type=pl.DeviceIdType.MESH)
-    pl.semaphore_wait(barrier, 2)
     for i in range(2):
         x_copy(i).wait()
 
     low = lax.broadcasted_iota(jnp.int32, (MINI_BATCH, 128), 1) < 64
 
-    def whole_tile(c):
+    def rows_of(b, j):
+        start = b * tok_dev + j * MINI_BATCH
+        return pl.ds(start if isinstance(start, int) else pl.multiple_of(start, MINI_BATCH), MINI_BATCH)
+
+    def multiply(g, b, j, with_k, with_q):
+        k_rows = rows = per_head_rows(kvq_buf[0, g, rows_of(b, j), :], low) if with_k else []
+        if with_q:
+            rows = rows + per_head_rows(kvq_buf[2, g, rows_of(b, j - 1), :], low)
+        prod = times_w(rows, w_now[b] if with_k and with_q or not with_k else w_buf[g, b])
+        if with_k:
+            z_buf[b] = own_columns(prod, low, 0)
+        if with_q:
+            o_buf[rows_of(b, j - 1), :] = own_columns(prod, low, 4 * MINI_BATCH if with_k else 0).astype(bf16)
+        return k_rows
+
+    def whole_tile(c, group=None):
         kind, g = tile_at(c)
         slot = lax.rem(c, 2)
         wait_theta(c)
         start_theta(c + 1)
         for i in range(2):
             rows = pl.ds(i * (n_rows // 2), n_rows // 2)
-            kvq_buf[kind, g, rows, :] = jnp.dot(x_buf[rows, :], theta_buf[slot], preferred_element_type=f32).astype(bf16)
+            part = jnp.dot(x_buf[rows, :], theta_buf[slot], preferred_element_type=f32).astype(bf16)
+            if group is not None and i == 0:
+                last_results(group)
+                before = tile_at(c - 1)
+                kvq_buf[before[0], before[1]] = tile_buf[...]
+            kvq_buf[kind, g, rows, :] = part
 
     def out_tile(n):
         c = n_tiles + n
@@ -174,9 +193,8 @@
             w_buf[pl.ds(lax.rem(n, 2) * sum_slots + i * (sum_slots // 2), sum_slots // 2)] = part.reshape(sum_slots // 2, *w_buf.shape[1:])
         sum_copy(n).start()
 
-    def inner(g, first_time, c, fill, per_trip):
+    def inner(g, first_time, c):
         slot = lax.rem(jnp.where(c < n_tiles, c, c - 1), 2)
-        has_q = jnp.logical_not(first_time) | (g >= n_late)
 
         @pl.when(c < n_tiles)
         def _():
@@ -204,22 +222,7 @@
 
         eta = eta_ref[g]
 
-        def rows_of(b, j):
-            start = b * tok_dev + j * MINI_BATCH
-            return pl.ds(start if isinstance(start, int) else pl.multiple_of(start, MINI_BATCH), MINI_BATCH)
-
         half = n_batch // 2
-
-        def multiply(b, j, with_k, with_q):
-            k_rows = rows = per_head_rows(kvq_buf[0, g, rows_of(b, j), :], low) if with_k else []
-            if with_q:
-                rows = rows + per_head_rows(kvq_buf[2, g, rows_of(b, j - 1), :], low)
-            prod = times_w(rows, w_now[b] if with_k and with_q or not with_k else w_buf[g, b])
-            if with_k:
-                z_buf[b] = own_columns(prod, low, 0)
-            if with_q:
-                o_buf[rows_of(b, j - 1), :] = own_columns(prod, low, 4 * MINI_BATCH if with_k else 0).astype(bf16)
-            return k_rows
 
         def update(b, j, k_rows=None, first=False):
             k_rows = k_rows or per_head_rows(kvq_buf[0, g, rows_of(b, j), :], low)
@@ -228,26 +231,22 @@
 
         def step(j, first=False, second=False):
             part = pl.ds(j * chunk if isinstance(j, int) else pl.multiple_of(j * chunk, chunk), chunk)
-            tile_part = jnp.dot(x_buf[part, :fill], theta_buf[slot, :fill, :], preferred_element_type=f32)
+            tile_part = jnp.dot(x_buf[part, :], theta_buf[slot], preferred_element_type=f32)
             k_rows = {}
             for b in range(half):
-                k_rows[b] = multiply(b, j, True, not first)
+                k_rows[b] = multiply(g, b, j, True, not first)
                 if not first:
                     update(half + b, j - 1, first=second)
             for b in range(half):
-                multiply(half + b, j, True, not first)
+                multiply(g, half + b, j, True, not first)
                 update(b, j, k_rows[b], first)
             tile_buf[part, :] = tile_part.astype(bf16)
 
         step(0, first=True)
         step(1, second=True)
 
-        def later_steps(i, _):
-            for s in range(per_trip):
-                step(2 + i * per_trip + s)
-            return 0
-
-        lax.fori_loop(0, (n_steps - 2) // per_trip, later_steps, 0)
+        for j in range(2, n_steps):
+            step(j)
         for b in range(half):
             update(half + b, n_steps - 1)
 
@@ -260,23 +259,21 @@
             w_send[...] = w_now[...]
             hand_on(g).start()
 
+    def last_results(g):
         for b in range(n_batch):
-            multiply(b, n_steps, False, True)
-
-        @pl.when(has_q & (g >= N_FIRST))
+            multiply(g, b, n_steps, False, True)
+        kvq_buf[2, g] = o_buf[...]
+
+    def send_result(g, first_time):
+        @pl.when((g >= N_FIRST) & (jnp.logical_not(first_time) | (g >= n_late)))
         def _():
             result(g).start()
 
-        @pl.when(has_q & (g < N_FIRST))
-        def _():
-            kvq_buf[2, g] = o_buf[...]
-
-        @pl.when(c < n_tiles)
-        def _():
-            kind, of = tile_at(c)
-            kvq_buf[kind, of] = tile_buf[...]
-
     def slot_body(s, _):
+        @pl.when(s == 1)
+        def _():
+            pl.semaphore_wait(barrier, 2)
+
         first_time = s <= n_groups + lag
         g = jnp.where(first_time, s - 1 - lag, s - (n_groups + 1 + lag))
         fresh = s < n_groups
@@ -289,13 +286,24 @@
 
         lax.fori_loop(jnp.where(first_time, outs_before(g - 1), 0), n_out, outs, 0)
 
-        @pl.when((g >= 0) & (c < n_tiles))
-        def _():
-            inner(g, first_time, c + n_out, depth, (n_steps - 2) // 2)
-
-        @pl.when((g >= 0) & (c >= n_tiles))
-        def _():
-            inner(g, first_time, c + n_out, FILL, (n_steps - 2) // 2)
+        @pl.when(g >= 0)
+        def _():
+            inner(g, first_time, c + n_out)
+
+        @pl.when((g >= 0) & fresh)
+        def _():
+            whole_tile(c + 1, g)
+            send_result(g, first_time)
+
+        @pl.when((g >= 0) & jnp.logical_not(fresh))
+        def _():
+            last_results(g)
+            send_result(g, first_time)
+
+            @pl.when(c < n_tiles)
+            def _():
+                kind, of = tile_at(c)
+                kvq_buf[kind, of] = tile_buf[...]
 
         def rest(i, _):
             whole_tile(c + i)
@@ -303,7 +311,7 @@
 
         @pl.when(fresh)
         def _():
-            lax.fori_loop(jnp.where(g >= 0, 1, 0), jnp.where(s < n_late, 2, 3), rest, 0)
+            lax.fori_loop(jnp.where(g >= 0, 2, 0), jnp.where(s < n_late, 2, 3), rest, 0)
         return 0
 
     lax.fori_loop(0, n_groups + 1 + lag + n_late, slot_body, 0)
@@ -323,6 +331,15 @@
     @pl.when(me < n_seq - 1)
     def _():
         hand_on(0).wait_send()
+
+
+def rest_kernel(o_ref, w_ref, sum_ref, out_ref):
+    n_rows = o_ref.shape[0]
+    slots = sum_ref.shape[0] // 2
+    for i in range(2):
+        rows = pl.ds(i * (n_rows // 2), n_rows // 2)
+        first = sum_ref[pl.ds(i * slots, slots)].reshape(n_rows // 2, out_ref.shape[1])
+        out_ref[rows, :] = (jnp.dot(o_ref[rows, :], w_ref[...], preferred_element_type=f32) + first).astype(bf16)
 
 
 def solution(mesh):
@@ -351,8 +368,18 @@
             compiler_params=pltpu.CompilerParams(collective_id=0, has_side_effects=True, vmem_limit_bytes=67043328),
             name="fused",
         )(flat, theta_k, theta_v, theta_q, w_out, w_init, eta)
-        rest = jnp.dot(o, w_out[256 * N_FIRST:], preferred_element_type=f32)
-        result = (rest + first_sum.reshape(n_rows, width_d)).astype(bf16)
+        depth = width - 256 * N_FIRST
+        result = pl.pallas_call(
+            rest_kernel,
+            out_shape=jax.ShapeDtypeStruct((n_rows, width_d), bf16),
+            grid=(width_d // REST_COLUMNS,),
+            in_specs=[pl.BlockSpec((n_rows, depth), lambda n: (0, 0), pipeline_mode=pl.Buffered(1)),
+                      pl.BlockSpec((depth, REST_COLUMNS), lambda n: (256 * N_FIRST // depth, n)),
+                      pl.BlockSpec((sum_slots, n_batch, head_dim, REST_COLUMNS), lambda n: (0, 0, 0, n))],
+            out_specs=pl.BlockSpec((n_rows, REST_COLUMNS), lambda n: (0, n)),
+            compiler_params=pltpu.CompilerParams(vmem_limit_bytes=48 * 1024 * 1024),
+            name="rest",
+        )(o, w_out, first_sum)
         return result.reshape(n_batch, tok_dev, width_d)
 
     tok_spec = P("data", "seq", None)

time: 296 us -> 290 us (0.980)
  matrix products: 21.9 us -> 0 us
  Pallas kernels: 272 us -> 286 us
    dot_general x1 -> x0, matrix products: 21.9 us -> none  [per_device(): rest = jnp.dot(o, w_out[256 * N_FIRST:], preferred_element_type=f32)]
    pallas_call x0 -> x1, Pallas kernels: none -> 20.1 us  [per_device(): pl.pallas_call(rest_kernel, out_shape=jax.ShapeDtypeStruct((n_rows, width...]
    pallas_call x1, Pallas kernels: 272 us -> 266 us  [per_device(): pl.pallas_call(functools.partial(fused_kernel, n_seq, n_batch, tok_dev, n...]
where the time goes in v8:
time: 290 us
  Pallas kernels  286 us (99%)
  local copies, waits for them, and re-layouts  3.04 us (1%)
    pallas_call x1, Pallas kernels, per_device(): pl.pallas_call(functools.partial(fused_kernel, n_seq, n_batch, tok_dev, n...  266 us
    pallas_call x1, Pallas kernels, per_device(): pl.pallas_call(rest_kernel, out_shape=jax.ShapeDtypeStruct((n_rows, width...  20.1 us

profile of v8, /device:TPU:127, one launch (start us, length us, event | category | flops | bytes accessed | tf_op | source)
XLA Modules:
  0.0 289.5 jit_solution(12625939027437683250)
XLA Ops:
  0.0 0.7 broadcast_multiply_fusion
  0.7 0.1 broadcast_in_dim.7
  0.7 0.1 broadcast_in_dim.8
  0.8 0.7 broadcast_in_dim.9.eta_ref
  1.5 265.7 %fused.1 = (bf16[2048,1024]{1,0:T(8,128)(2,1)}, f32[4,8,64,3072]{3,2,1,0:T(8,128)}) custom-call(bf16[2048,3072]{1,0:T(8,128)(2,1)} %bitcast.2, bf16[3072,3072]{1,0:T(8,128)(2,1)} %theta_k_hbm.1, bf16[3072,3072]{1,0:T(8,128)(2,1)} %theta_v_hbm.1, bf16[3072,3072]{1,0:T(8,128)(2,1)} %theta_q_hbm.1, bf16[3072,3072]{1,0:T(8,128)(2,1)} %w_ref.1, ...), custom_call_target="tpu_custom_call" | custom-call | tf_op jit(solution)/shard_map/fused/pallas_call | solution.py:357
  267.2 0.0 copy-start
  267.2 2.2 copy-done
  269.4 20.1 %rest.1 = bf16[2048,3072]{1,0:T(8,128)(2,1)} custom-call(bf16[2048,1024]{1,0:T(8,128)(2,1)S(1)} %copy-done, bf16[3072,3072]{1,0:T(8,128)(2,1)} %w_ref.1, f32[4,8,64,3072]{3,2,1,0:T(8,128)} %get-tuple-element.8.sum_ref), custom_call_target="tpu_custom_call" | custom-call | tf_op jit(solution)/shard_map/rest/pallas_call | solution.py:372
Async XLA Ops:
  267.2 2.2 copy-start

commit v9 on v8

--- a/solution.py
+++ b/solution.py
@@ -60,7 +60,7 @@
     return jnp.dot(lhs, rhs, preferred_element_type=f32)
 
 
-def fused_kernel(n_seq, n_batch, tok_dev, n_groups, x_hbm, theta_k_hbm, theta_v_hbm, theta_q_hbm, w_out_hbm, w_init_hbm, eta_ref, o_hbm, sum_hbm,
+def fused_kernel(n_seq, n_batch, tok_dev, n_groups, x_hbm, theta_k_hbm, theta_v_hbm, theta_q_hbm, w_out_hbm, w_init_hbm, lr_ref, o_hbm, sum_hbm,
                  x_buf, kvq_buf, theta_buf, tile_buf, o_buf, z_buf, w_buf, w_now, w_send, init_buf, x_sem, theta_sem, out_sem, sum_sem, init_sem, send_sem, recv_sem):
     me = lax.axis_index("seq")
     lag, n_late = jnp.int32(0), jnp.int32(0)
@@ -146,6 +146,7 @@
         x_copy(i).wait()
 
     low = lax.broadcasted_iota(jnp.int32, (MINI_BATCH, 128), 1) < 64
+    head = lax.broadcasted_iota(jnp.int32, (1, 256), 1) // 64
 
     def rows_of(b, j):
         start = b * tok_dev + j * MINI_BATCH
@@ -220,7 +221,9 @@
         def _():
             result(N_FIRST).wait()
 
-        eta = eta_ref[g]
+        eta = jnp.zeros((1, 256), f32)
+        for h in range(HEADS_PER_GROUP):
+            eta = jnp.where(head == h, (2.0 / MINI_BATCH) * lr_ref[g * HEADS_PER_GROUP + h], eta)
 
         half = n_batch // 2
 
@@ -333,13 +336,70 @@
         hand_on(0).wait_send()
 
 
-def rest_kernel(o_ref, w_ref, sum_ref, out_ref):
-    n_rows = o_ref.shape[0]
-    slots = sum_ref.shape[0] // 2
+def rest_kernel(o_hbm, w_hbm, sum_hbm, out_hbm, o_buf, w_buf, sum_buf, out_buf, o_sem, w_sem, sum_sem, out_sem):
+    n_rows, depth = o_buf.shape
+    half, slots = n_rows // 2, sum_buf.shape[1] // 2
+    n_parts = out_hbm.shape[1] // REST_COLUMNS
+
+    def columns(n):
+        return pl.ds(pl.multiple_of(n * REST_COLUMNS, REST_COLUMNS), REST_COLUMNS)
+
+    def o_copy(i):
+        rows = pl.ds(i * half, half)
+        return pltpu.make_async_copy(o_hbm.at[rows], o_buf.at[rows], o_sem.at[i])
+
+    def w_copy(n):
+        slot = lax.rem(n, 2)
+        return pltpu.make_async_copy(w_hbm.at[pl.ds(w_hbm.shape[0] - depth, depth), columns(n)], w_buf.at[slot], w_sem.at[slot])
+
+    def sum_copy(n, i):
+        slot, part = lax.rem(n, 2), pl.ds(i * slots, slots)
+        return pltpu.make_async_copy(sum_hbm.at[part, :, :, columns(n)], sum_buf.at[slot, part], sum_sem.at[slot, i])
+
+    def out_copy(n, i):
+        slot, rows = lax.rem(n, 2), pl.ds(i * half, half)
+        return pltpu.make_async_copy(out_buf.at[slot, rows], out_hbm.at[rows, columns(n)], out_sem.at[slot, i])
+
+    first = jnp.int32(0)
+    w_copy(first).start()
     for i in range(2):
-        rows = pl.ds(i * (n_rows // 2), n_rows // 2)
-        first = sum_ref[pl.ds(i * slots, slots)].reshape(n_rows // 2, out_ref.shape[1])
-        out_ref[rows, :] = (jnp.dot(o_ref[rows, :], w_ref[...], preferred_element_type=f32) + first).astype(bf16)
+        o_copy(i).start()
+        sum_copy(first, i).start()
+    w_copy(first + 1).start()
+
+    def part(n, _):
+        slot = lax.rem(n, 2)
+        w_copy(n).wait()
+
+        @pl.when(n + 1 < n_parts)
+        def _():
+            for i in range(2):
+                sum_copy(n + 1, i).start()
+
+        for i in range(2):
+            @pl.when(n == 0)
+            def _():
+                o_copy(i).wait()
+
+            @pl.when(n >= 2)
+            def _():
+                out_copy(n - 2, i).wait()
+
+            sum_copy(n, i).wait()
+            rows = pl.ds(i * half, half)
+            so_far = sum_buf[slot, pl.ds(i * slots, slots)].reshape(half, REST_COLUMNS)
+            out_buf[slot, rows, :] = (jnp.dot(o_buf[rows, :], w_buf[slot], preferred_element_type=f32) + so_far).astype(bf16)
+            out_copy(n, i).start()
+
+        @pl.when(n + 2 < n_parts)
+        def _():
+            w_copy(n + 2).start()
+        return 0
+
+    lax.fori_loop(0, n_parts, part, 0)
+    for n in range(n_parts - 2, n_parts):
+        for i in range(2):
+            out_copy(n, i).wait()
 
 
 def solution(mesh):
@@ -351,13 +411,12 @@
         n_groups = n_heads // HEADS_PER_GROUP
         n_rows, width = n_batch * tok_dev, n_heads * head_dim
         flat = tokens.reshape(n_rows, width_d)
-        eta = jnp.repeat((2.0 / MINI_BATCH) * inner_lr, head_dim).reshape(n_groups, 1, 4 * head_dim)
-        hbm, vmem = pl.BlockSpec(memory_space=pl.ANY), pl.BlockSpec(memory_space=pltpu.VMEM)
+        hbm, smem = pl.BlockSpec(memory_space=pl.ANY), pl.BlockSpec(memory_space=pltpu.SMEM)
         sum_slots = n_rows // (n_batch * head_dim)
         o, first_sum = pl.pallas_call(
             functools.partial(fused_kernel, n_seq, n_batch, tok_dev, n_groups),
             out_shape=(jax.ShapeDtypeStruct((n_rows, width - 256 * N_FIRST), bf16), jax.ShapeDtypeStruct((sum_slots, n_batch, head_dim, width_d), f32)),
-            in_specs=[hbm] * 6 + [vmem], out_specs=(hbm, hbm),
+            in_specs=[hbm] * 6 + [smem], out_specs=(hbm, hbm),
             scratch_shapes=[pltpu.VMEM((n_rows, width_d), bf16), pltpu.VMEM((3, n_groups, n_rows, 256), bf16),
                             pltpu.VMEM((2, width_d, 256), bf16), pltpu.VMEM((n_rows, 256), bf16), pltpu.VMEM((n_rows, 256), bf16), pltpu.VMEM((n_batch, MINI_BATCH, 256), f32),
                             pltpu.VMEM((n_groups, n_batch, head_dim, 4 * head_dim), f32),
@@ -367,17 +426,16 @@
                             pltpu.SemaphoreType.DMA, pltpu.SemaphoreType.DMA, pltpu.SemaphoreType.DMA((n_groups,))],
             compiler_params=pltpu.CompilerParams(collective_id=0, has_side_effects=True, vmem_limit_bytes=67043328),
             name="fused",
-        )(flat, theta_k, theta_v, theta_q, w_out, w_init, eta)
+        )(flat, theta_k, theta_v, theta_q, w_out, w_init, inner_lr)
         depth = width - 256 * N_FIRST
         result = pl.pallas_call(
             rest_kernel,
             out_shape=jax.ShapeDtypeStruct((n_rows, width_d), bf16),
-            grid=(width_d // REST_COLUMNS,),
-            in_specs=[pl.BlockSpec((n_rows, depth), lambda n: (0, 0), pipeline_mode=pl.Buffered(1)),
-                      pl.BlockSpec((depth, REST_COLUMNS), lambda n: (256 * N_FIRST // depth, n)),
-                      pl.BlockSpec((sum_slots, n_batch, head_dim, REST_COLUMNS), lambda n: (0, 0, 0, n))],
-            out_specs=pl.BlockSpec((n_rows, REST_COLUMNS), lambda n: (0, n)),
-            compiler_params=pltpu.CompilerParams(vmem_limit_bytes=48 * 1024 * 1024),
+            in_specs=[hbm] * 3, out_specs=hbm,
+            scratch_shapes=[pltpu.VMEM((n_rows, depth), bf16), pltpu.VMEM((2, depth, REST_COLUMNS), bf16),
+                            pltpu.VMEM((2, sum_slots, n_batch, head_dim, REST_COLUMNS), f32), pltpu.VMEM((2, n_rows, REST_COLUMNS), bf16),
+                            pltpu.SemaphoreType.DMA((2,)), pltpu.SemaphoreType.DMA((2,)), pltpu.SemaphoreType.DMA((2, 2)), pltpu.SemaphoreType.DMA((2, 2))],
+            compiler_params=pltpu.CompilerParams(vmem_limit_bytes=67043328),
             name="rest",
         )(o, w_out, first_sum)
         return result.reshape(n_batch, tok_dev, width_d)

time: 290 us -> 285 us (0.983)
  local copies, waits for them, and re-layouts: 3.04 us -> 0 us
where the time goes in v9:
time: 285 us; the launch traced here: 284 us
  Pallas kernels  284 us (100%)
    pallas_call x1, Pallas kernels, per_device(): pl.pallas_call(functools.partial(fused_kernel, n_seq, n_batch, tok_dev, n...  266 us
    pallas_call x1, Pallas kernels, per_device(): pl.pallas_call(rest_kernel, out_shape=jax.ShapeDtypeStruct((n_rows, width...  18.7 us

profile of v9, /device:TPU:127, one launch (start us, length us, event | category | flops | bytes accessed | tf_op | source)
XLA Modules:
  0.0 284.5 jit_solution(13568399231642269119)
XLA Ops:
  0.0 265.6 %fused.1 = (bf16[2048,1024]{1,0:T(8,128)(2,1)}, f32[4,8,64,3072]{3,2,1,0:T(8,128)}) custom-call(bf16[2048,3072]{1,0:T(8,128)(2,1)} %bitcast.2, bf16[3072,3072]{1,0:T(8,128)(2,1)} %theta_k_hbm.1, bf16[3072,3072]{1,0:T(8,128)(2,1)} %theta_v_hbm.1, bf16[3072,3072]{1,0:T(8,128)(2,1)} %theta_q_hbm.1, bf16[3072,3072]{1,0:T(8,128)(2,1)} %w_hbm.1, ...), custom_call_target="tpu_custom_call" | custom-call | tf_op jit(solution)/shard_map/fused/pallas_call | solution.py:416
  265.6 18.7 %rest.1 = bf16[2048,3072]{1,0:T(8,128)(2,1)} custom-call(bf16[2048,1024]{1,0:T(8,128)(2,1)} %get-tuple-element.7.o_hbm, bf16[3072,3072]{1,0:T(8,128)(2,1)} %w_hbm.1, f32[4,8,64,3072]{3,2,1,0:T(8,128)} %get-tuple-element.8.sum_hbm), custom_call_target="tpu_custom_call" | custom-call | tf_op jit(solution)/shard_map/rest/pallas_call | solution.py:431

commit v10 on v9

--- a/solution.py
+++ b/solution.py
@@ -9,8 +9,8 @@
 
 MINI_BATCH = 16
 HEADS_PER_GROUP = 4
-SCHEDULE = ((0, 6, (0, 0, 0, 0)), (1, 5, (0, 0, 0, 0)), (2, 4, (0, 0, 0, 0)), (2, 4, (0, 0, 0, 0)),
-            (5, 2, (0, 0, 0, 0)), (5, 0, (4, 8, 8, 9)), (7, 0, (8, 8, 11, 11)), (7, 0, (10, 11, 11, 11)))
+SCHEDULE = ((0, 5, (0, 0, 0, 0)), (1, 4, (0, 0, 0, 0)), (2, 1, (0, 0, 0, 0)), (2, 0, (0, 0, 0, 0)),
+            (4, 0, (3, 6, 6, 6)), (5, 0, (3, 6, 6, 6)), (5, 0, (4, 6, 6, 6)), (8, 0, (6, 6, 6, 6)))
 N_FIRST = 8
 REST_COLUMNS = 512
 bf16, f32 = jnp.bfloat16, jnp.float32
@@ -23,50 +23,58 @@
     return a, b, (rest - b.astype(f32)).astype(bf16)
 
 
-def per_head_rows(x, low):
+def per_head_rows(x):
     rows = []
     for half in range(2):
-        y = x[:, half * 128:(half + 1) * 128]
-        turned = pltpu.roll(y, 64, 1)
+        y = x[:, :, half * 128:(half + 1) * 128]
+        turned, low = pltpu.roll(y, 64, 2), low_lanes(y.shape)
         rows += [jnp.where(low, y, turned), jnp.where(low, turned, y)]
     return rows
 
 
-def own_columns(z, low, first):
-    t = MINI_BATCH
-    return jnp.concatenate([
-        jnp.where(low, z[first:first + t, :128], z[first + t:first + 2 * t, :128]),
-        jnp.where(low, z[first + 2 * t:first + 3 * t, 128:], z[first + 3 * t:first + 4 * t, 128:])], axis=1)
+def low_lanes(shape):
+    return lax.broadcasted_iota(jnp.int32, shape, 2) < 64
+
+
+def under(rows):
+    n, t, width = rows[0].shape
+    return jnp.concatenate([r.reshape(n, 1, t, width) for r in rows], axis=1).reshape(n, t * len(rows), width)
+
+
+def own_columns(z, first):
+    a, b, c, d = (z[:, first + i * MINI_BATCH:first + (i + 1) * MINI_BATCH, (i // 2) * 128:(i // 2 + 1) * 128] for i in range(4))
+    low = low_lanes(a.shape)
+    return jnp.concatenate([jnp.where(low, a, b), jnp.where(low, c, d)], axis=2)
 
 
 def times_w(rows, w):
-    m = jnp.concatenate(rows, axis=0)
-    lhs = jnp.concatenate([m, m], axis=1)
-    rhs = jnp.concatenate([*split3(w), jnp.zeros(w.shape, bf16)], axis=0)
-    return jnp.dot(lhs, rhs, preferred_element_type=f32)
-
-
-def k_transposed_times(k_rows, r, low):
-    zero = jnp.zeros((MINI_BATCH, 128), bf16)
+    m = under(rows)
+    return jnp.concatenate([m, m], axis=2), jnp.concatenate([*split3(w), jnp.zeros(w.shape, bf16)], axis=1)
+
+
+def k_transposed_times(k_rows, r):
+    zero = jnp.zeros((*r.shape[:2], 128), bf16)
+    low = low_lanes(zero.shape)
     rows = []
     for part in split3(r):
-        a, b = part[:, :128], part[:, 128:]
-        rows += [jnp.concatenate([jnp.where(low, a, zero), zero], axis=1), jnp.concatenate([jnp.where(low, zero, a), zero], axis=1),
-                 jnp.concatenate([zero, jnp.where(low, b, zero)], axis=1), jnp.concatenate([zero, jnp.where(low, zero, b)], axis=1)]
-    rhs = jnp.concatenate([*rows, jnp.zeros((4 * MINI_BATCH, 256), bf16)], axis=0)
-    k_mat = jnp.concatenate(k_rows, axis=0)
-    turned = jnp.concatenate([k_mat, k_mat], axis=0).T[:64]
-    lhs = jnp.concatenate([turned, turned], axis=1)
-    return jnp.dot(lhs, rhs, preferred_element_type=f32)
+        a, b = part[:, :, :128], part[:, :, 128:]
+        rows += [jnp.concatenate(pair, axis=2) for pair in (
+            (jnp.where(low, a, zero), zero), (jnp.where(low, zero, a), zero), (zero, jnp.where(low, b, zero)), (zero, jnp.where(low, zero, b)))]
+    rhs = jnp.concatenate([under(rows), jnp.zeros((r.shape[0], 4 * MINI_BATCH, 256), bf16)], axis=1)
+    twice = under(k_rows + k_rows)
+    turned = [twice[i].T[:64] for i in range(r.shape[0])]
+    return [jnp.concatenate([t, t], axis=1) for t in turned], rhs
 
 
 def fused_kernel(n_seq, n_batch, tok_dev, n_groups, x_hbm, theta_k_hbm, theta_v_hbm, theta_q_hbm, w_out_hbm, w_init_hbm, lr_ref, o_hbm, sum_hbm,
-                 x_buf, kvq_buf, theta_buf, tile_buf, o_buf, z_buf, w_buf, w_now, w_send, init_buf, x_sem, theta_sem, out_sem, sum_sem, init_sem, send_sem, recv_sem):
+                 x_buf, kvq_buf, theta_buf, tile_buf, o_buf, w_buf, w_now, w_send, init_buf, x_sem, theta_sem, out_sem, sum_sem, init_sem, send_sem, recv_sem):
     me = lax.axis_index("seq")
     lag, n_late = jnp.int32(0), jnp.int32(0)
     for place, (ahead, late, _) in enumerate(SCHEDULE):
         lag = jnp.where(me == place, ahead, lag)
         n_late = jnp.where(me == place, late, n_late)
+
+    outs_beside = (n_late == 0) & (lag > 2)
 
     def outs_before(g):
         n = jnp.int32(0)
@@ -113,7 +121,7 @@
         pltpu.make_async_copy(theta_k_hbm.at[:, pl.ds(0, 256)], theta_buf.at[slot], theta_sem.at[slot]).wait()
 
     def result(g):
-        return pltpu.make_async_copy(o_buf, o_hbm.at[:, columns(g - N_FIRST)], out_sem)
+        return pltpu.make_async_copy(o_buf, o_hbm.at[:, :, columns(g - N_FIRST)], out_sem)
 
     def sum_copy(n):
         part = lax.rem(n, 2)
@@ -142,26 +150,49 @@
 
     for peer in (lax.rem(me + 1, n_seq), lax.rem(me + n_seq - 1, n_seq)):
         pl.semaphore_signal(barrier, inc=1, device_id={"seq": peer}, device_id_type=pl.DeviceIdType.MESH)
-    for i in range(2):
-        x_copy(i).wait()
-
-    low = lax.broadcasted_iota(jnp.int32, (MINI_BATCH, 128), 1) < 64
+
     head = lax.broadcasted_iota(jnp.int32, (1, 256), 1) // 64
 
-    def rows_of(b, j):
-        start = b * tok_dev + j * MINI_BATCH
-        return pl.ds(start if isinstance(start, int) else pl.multiple_of(start, MINI_BATCH), MINI_BATCH)
-
-    def multiply(g, b, j, with_k, with_q):
-        k_rows = rows = per_head_rows(kvq_buf[0, g, rows_of(b, j), :], low) if with_k else []
-        if with_q:
-            rows = rows + per_head_rows(kvq_buf[2, g, rows_of(b, j - 1), :], low)
-        prod = times_w(rows, w_now[b] if with_k and with_q or not with_k else w_buf[g, b])
-        if with_k:
-            z_buf[b] = own_columns(prod, low, 0)
-        if with_q:
-            o_buf[rows_of(b, j - 1), :] = own_columns(prod, low, 4 * MINI_BATCH if with_k else 0).astype(bf16)
-        return k_rows
+    half = n_batch // 2
+
+    def tokens(kind, g, units, j):
+        return kvq_buf[kind, g, units, pl.ds(j * MINI_BATCH, MINI_BATCH), :]
+
+    def chain_step(g, eta, j, now, before):
+        k_rows = z = None
+        if now is not None:
+            k_rows = per_head_rows(tokens(0, g, now, j)) if j < n_steps else []
+            rows = k_rows + (per_head_rows(tokens(2, g, now, j - 1)) if j > 0 else [])
+            lhs, rhs = times_w(rows, w_now[now])
+        if before is not None:
+            units, step, keys, inputs = before
+            r = (inputs - tokens(1, g, units, step).astype(f32)) * eta
+            lhs_u, rhs_u = k_transposed_times(keys, r)
+        prod, change = [], []
+        for i in range(half):
+            if now is not None:
+                prod.append(jnp.dot(lhs[i], rhs[i], preferred_element_type=f32))
+            if before is not None:
+                change.append(jnp.dot(lhs_u[i], rhs_u[i], preferred_element_type=f32))
+        if now is not None:
+            prod = jnp.stack(prod)
+            if j < n_steps:
+                z = own_columns(prod, 0)
+            if j > 0:
+                o_buf[now, pl.ds((j - 1) * MINI_BATCH, MINI_BATCH), :] = own_columns(prod, 4 * MINI_BATCH if j < n_steps else 0).astype(bf16)
+        if before is not None:
+            w_now[units] = w_now[units] - jnp.stack(change)
+        return k_rows, z
+
+    def chain(g, eta, fill):
+        one, two = pl.ds(0, half), pl.ds(half, half)
+        open_two = None
+        for j in range(n_steps):
+            put = fill(j)
+            open_one = (one, j, *chain_step(g, eta, j, one, open_two))
+            open_two = (two, j, *chain_step(g, eta, j, two, open_one))
+            put()
+        chain_step(g, eta, n_steps, None, open_two)
 
     def whole_tile(c, group=None):
         kind, g = tile_at(c)
@@ -170,12 +201,14 @@
         start_theta(c + 1)
         for i in range(2):
             rows = pl.ds(i * (n_rows // 2), n_rows // 2)
+            if isinstance(c, int):
+                x_copy(i).wait()
             part = jnp.dot(x_buf[rows, :], theta_buf[slot], preferred_element_type=f32).astype(bf16)
             if group is not None and i == 0:
                 last_results(group)
                 before = tile_at(c - 1)
-                kvq_buf[before[0], before[1]] = tile_buf[...]
-            kvq_buf[kind, g, rows, :] = part
+                kvq_buf[before[0], before[1]] = tile_buf[...].reshape(n_batch, tok_dev, 256)
+            kvq_buf[kind, g, pl.ds(i * half, half)] = part.reshape(half, tok_dev, 256)
 
     def out_tile(n):
         c = n_tiles + n
@@ -189,18 +222,26 @@
 
         for i in range(2):
             rows = pl.ds(i * (n_rows // 2), n_rows // 2)
-            lhs = jnp.concatenate([kvq_buf[2, g, rows, :] for g in range(N_FIRST)], axis=1)
+            lhs = jnp.concatenate([kvq_buf[2, g, pl.ds(i * half, half)].reshape(n_rows // 2, 256) for g in range(N_FIRST)], axis=1)
             part = jnp.dot(lhs, theta_buf[slot, :first_depth, :], preferred_element_type=f32)
             w_buf[pl.ds(lax.rem(n, 2) * sum_slots + i * (sum_slots // 2), sum_slots // 2)] = part.reshape(sum_slots // 2, *w_buf.shape[1:])
         sum_copy(n).start()
 
-    def inner(g, first_time, c):
-        slot = lax.rem(jnp.where(c < n_tiles, c, c - 1), 2)
-
-        @pl.when(c < n_tiles)
-        def _():
-            wait_theta(c)
+    def inner(g, first_time, c, n=None):
+        slot = lax.rem(jnp.where(c < n_tiles, c, c - 1), 2) if n is None else lax.rem(c, 2)
+
+        if n is None:
+            @pl.when(c < n_tiles)
+            def _():
+                wait_theta(c)
+                start_theta(c + 1)
+        else:
+            w_out_copy(n, slot).wait()
             start_theta(c + 1)
+
+            @pl.when(n >= 2)
+            def _():
+                sum_copy(n - 2).wait()
 
         @pl.when((me == 0) & first_time)
         def _():
@@ -225,33 +266,32 @@
         for h in range(HEADS_PER_GROUP):
             eta = jnp.where(head == h, (2.0 / MINI_BATCH) * lr_ref[g * HEADS_PER_GROUP + h], eta)
 
-        half = n_batch // 2
-
-        def update(b, j, k_rows=None, first=False):
-            k_rows = k_rows or per_head_rows(kvq_buf[0, g, rows_of(b, j), :], low)
-            r = (z_buf[b] - kvq_buf[1, g, rows_of(b, j), :].astype(f32)) * eta
-            w_now[b] = (w_buf[g, b] if first else w_now[b]) - k_transposed_times(k_rows, r, low)
-
-        def step(j, first=False, second=False):
-            part = pl.ds(j * chunk if isinstance(j, int) else pl.multiple_of(j * chunk, chunk), chunk)
-            tile_part = jnp.dot(x_buf[part, :], theta_buf[slot], preferred_element_type=f32)
-            k_rows = {}
-            for b in range(half):
-                k_rows[b] = multiply(g, b, j, True, not first)
-                if not first:
-                    update(half + b, j - 1, first=second)
-            for b in range(half):
-                multiply(g, half + b, j, True, not first)
-                update(b, j, k_rows[b], first)
-            tile_buf[part, :] = tile_part.astype(bf16)
-
-        step(0, first=True)
-        step(1, second=True)
-
-        for j in range(2, n_steps):
-            step(j)
-        for b in range(half):
-            update(half + b, n_steps - 1)
+        w_now[...] = w_buf[g]
+
+        if n is None:
+            def fill(j):
+                part = pl.ds(j * chunk, chunk)
+                tile_part = jnp.dot(x_buf[part, :], theta_buf[slot], preferred_element_type=f32)
+
+                def put():
+                    tile_buf[part, :] = tile_part.astype(bf16)
+                return put
+        else:
+            def fill(j):
+                b, first = j * chunk // tok_dev, j * chunk % tok_dev
+                lhs = jnp.concatenate([kvq_buf[2, i, b, pl.ds(first, chunk), :] for i in range(N_FIRST)], axis=1)
+                part = jnp.dot(lhs, theta_buf[slot, :first_depth, :], preferred_element_type=f32)
+                rows = n_batch * w_buf.shape[2]
+                at, within = j * chunk // rows, j * chunk % rows // w_buf.shape[2]
+
+                def put():
+                    w_buf[lax.rem(n, 2) * sum_slots + at, pl.ds(within, chunk // w_buf.shape[2])] = part.reshape(chunk // w_buf.shape[2], *w_buf.shape[2:])
+                return put
+
+        chain(g, eta, fill)
+
+        if n is not None:
+            sum_copy(n).start()
 
         @pl.when((me < n_seq - 1) & first_time & (g > 0))
         def _():
@@ -263,8 +303,8 @@
             hand_on(g).start()
 
     def last_results(g):
-        for b in range(n_batch):
-            multiply(g, b, n_steps, False, True)
+        for units in (pl.ds(0, half), pl.ds(half, half)):
+            chain_step(g, None, n_steps, units, None)
         kvq_buf[2, g] = o_buf[...]
 
     def send_result(g, first_time):
@@ -281,17 +321,22 @@
         g = jnp.where(first_time, s - 1 - lag, s - (n_groups + 1 + lag))
         fresh = s < n_groups
         c = jnp.where(fresh, 2 * s + jnp.maximum(s - n_late, 0), jnp.minimum(n_tiles - n_late + s - n_groups, n_tiles))
-        n_out = jnp.where(first_time, outs_before(g), 0)
+        beside_out = outs_beside & first_time & (g >= N_FIRST)
+        n_out = jnp.where(beside_out, outs_before(g) + g - N_FIRST, 0)
 
         def outs(n, _):
             out_tile(n)
             return 0
 
-        lax.fori_loop(jnp.where(first_time, outs_before(g - 1), 0), n_out, outs, 0)
-
-        @pl.when(g >= 0)
-        def _():
-            inner(g, first_time, c + n_out)
+        lax.fori_loop(jnp.where(beside_out, outs_before(g - 1) + g - N_FIRST, 0), n_out, outs, 0)
+
+        @pl.when((g >= 0) & jnp.logical_not(beside_out))
+        def _():
+            inner(g, first_time, c)
+
+        @pl.when(beside_out)
+        def _():
+            inner(g, first_time, n_tiles + n_out, n_out)
 
         @pl.when((g >= 0) & fresh)
         def _():
@@ -306,7 +351,7 @@
             @pl.when(c < n_tiles)
             def _():
                 kind, of = tile_at(c)
-                kvq_buf[kind, of] = tile_buf[...]
+                kvq_buf[kind, of] = tile_buf[...].reshape(n_batch, tok_dev, 256)
 
         def rest(i, _):
             whole_tile(c + i)
@@ -314,16 +359,17 @@
 
         @pl.when(fresh)
         def _():
-            lax.fori_loop(jnp.where(g >= 0, 2, 0), jnp.where(s < n_late, 2, 3), rest, 0)
+            lax.fori_loop(jnp.where(g >= 0, 2, jnp.where(s == 0, 1, 0)), jnp.where(s < n_late, 2, 3), rest, 0)
         return 0
 
+    whole_tile(0)
     lax.fori_loop(0, n_groups + 1 + lag + n_late, slot_body, 0)
 
     def outs(n, _):
         out_tile(n)
         return 0
 
-    lax.fori_loop(outs_before(n_groups), n_out_tiles, outs, 0)
+    lax.fori_loop(jnp.where(outs_beside, outs_before(n_groups) + n_groups - N_FIRST, 0), n_out_tiles, outs, 0)
     for n in range(2):
         sum_copy(n_out_tiles - 2 + n).wait()
 
@@ -415,10 +461,10 @@
         sum_slots = n_rows // (n_batch * head_dim)
         o, first_sum = pl.pallas_call(
             functools.partial(fused_kernel, n_seq, n_batch, tok_dev, n_groups),
-            out_shape=(jax.ShapeDtypeStruct((n_rows, width - 256 * N_FIRST), bf16), jax.ShapeDtypeStruct((sum_slots, n_batch, head_dim, width_d), f32)),
+            out_shape=(jax.ShapeDtypeStruct((n_batch, tok_dev, width - 256 * N_FIRST), bf16), jax.ShapeDtypeStruct((sum_slots, n_batch, head_dim, width_d), f32)),
             in_specs=[hbm] * 6 + [smem], out_specs=(hbm, hbm),
-            scratch_shapes=[pltpu.VMEM((n_rows, width_d), bf16), pltpu.VMEM((3, n_groups, n_rows, 256), bf16),
-                            pltpu.VMEM((2, width_d, 256), bf16), pltpu.VMEM((n_rows, 256), bf16), pltpu.VMEM((n_rows, 256), bf16), pltpu.VMEM((n_batch, MINI_BATCH, 256), f32),
+            scratch_shapes=[pltpu.VMEM((n_rows, width_d), bf16), pltpu.VMEM((3, n_groups, n_batch, tok_dev, 256), bf16),
+                            pltpu.VMEM((2, width_d, 256), bf16), pltpu.VMEM((n_rows, 256), bf16), pltpu.VMEM((n_batch, tok_dev, 256), bf16),
                             pltpu.VMEM((n_groups, n_batch, head_dim, 4 * head_dim), f32),
                             pltpu.VMEM((n_batch, head_dim, 4 * head_dim), f32), pltpu.VMEM((n_batch, head_dim, 4 * head_dim), f32),
                             pltpu.VMEM((HEADS_PER_GROUP, head_dim, head_dim), f32),
@@ -437,7 +483,7 @@
                             pltpu.SemaphoreType.DMA((2,)), pltpu.SemaphoreType.DMA((2,)), pltpu.SemaphoreType.DMA((2, 2)), pltpu.SemaphoreType.DMA((2, 2))],
             compiler_params=pltpu.CompilerParams(vmem_limit_bytes=67043328),
             name="rest",
-        )(o, w_out, first_sum)
+        )(o.reshape(n_rows, depth), w_out, first_sum)
         return result.reshape(n_batch, tok_dev, width_d)
 
     tok_spec = P("data", "seq", None)

time: 285 us -> 281 us (0.986)
  Pallas kernels: 284 us -> 281 us
    pallas_call x1, Pallas kernels: 266 us -> 262 us  [per_device(): pl.pallas_call(functools.partial(fused_kernel, n_seq, n_batch, tok_dev, n...]
where the time goes in v10:
time: 281 us
  Pallas kernels  281 us (100%)
    pallas_call x1, Pallas kernels, per_device(): pl.pallas_call(functools.partial(fused_kernel, n_seq, n_batch, tok_dev, n...  262 us
    pallas_call x1, Pallas kernels, per_device(): pl.pallas_call(rest_kernel, out_shape=jax.ShapeDtypeStruct((n_rows, width...  18.7 us

profile of v10, /device:TPU:127, one launch (start us, length us, event | category | flops | bytes accessed | tf_op | source)
XLA Modules:
  0.0 280.9 jit_solution(3640655979473253577)
XLA Ops:
  0.0 262.0 %fused.1 = (bf16[8,256,1024]{2,1,0:T(8,128)(2,1)}, f32[4,8,64,3072]{3,2,1,0:T(8,128)}) custom-call(bf16[2048,3072]{1,0:T(8,128)(2,1)} %bitcast.3, bf16[3072,3072]{1,0:T(8,128)(2,1)} %theta_k_hbm.1, bf16[3072,3072]{1,0:T(8,128)(2,1)} %theta_v_hbm.1, bf16[3072,3072]{1,0:T(8,128)(2,1)} %theta_q_hbm.1, bf16[3072,3072]{1,0:T(8,128)(2,1)} %w_hbm.1, ...), custom_call_target="tpu_custom_call" | custom-call | tf_op jit(solution)/shard_map/fused/pallas_call | solution.py:462
  262.0 18.7 %rest.1 = bf16[2048,3072]{1,0:T(8,128)(2,1)} custom-call(bf16[2048,1024]{1,0:T(8,128)(2,1)} %bitcast.4, bf16[3072,3072]{1,0:T(8,128)(2,1)} %w_hbm.1, f32[4,8,64,3072]{3,2,1,0:T(8,128)} %get-tuple-element.8.sum_hbm), custom_call_target="tpu_custom_call" | custom-call | tf_op jit(solution)/shard_map/rest/pallas_call | solution.py:477

commit v11 on v10

--- a/solution.py
+++ b/solution.py
@@ -9,9 +9,9 @@
 
 MINI_BATCH = 16
 HEADS_PER_GROUP = 4
-SCHEDULE = ((0, 5, (0, 0, 0, 0)), (1, 4, (0, 0, 0, 0)), (2, 1, (0, 0, 0, 0)), (2, 0, (0, 0, 0, 0)),
-            (4, 0, (3, 6, 6, 6)), (5, 0, (3, 6, 6, 6)), (5, 0, (4, 6, 6, 6)), (8, 0, (6, 6, 6, 6)))
-N_FIRST = 8
+SCHEDULE = ((0, 6, (0, 0, 0, 0, 0)), (1, 5, (0, 0, 0, 0, 0)), (3, 3, (0, 0, 0, 0, 0)), (3, 1, (0, 0, 0, 0, 0)),
+            (4, 0, (0, 3, 3, 3, 3)), (5, 0, (3, 6, 6, 6, 6)), (5, 0, (3, 6, 6, 6, 6)), (5, 0, (3, 6, 6, 7, 7)))
+N_FIRST = 7
 REST_COLUMNS = 512
 bf16, f32 = jnp.bfloat16, jnp.float32
 
@@ -74,7 +74,7 @@
         lag = jnp.where(me == place, ahead, lag)
         n_late = jnp.where(me == place, late, n_late)
 
-    outs_beside = (n_late == 0) & (lag > 2)
+    outs_beside = (n_late == 0) & (lag + 1 + N_FIRST >= n_groups)
 
     def outs_before(g):
         n = jnp.int32(0)
@@ -85,6 +85,7 @@
 
     n_tiles = 3 * n_groups
     n_out_tiles = sum_hbm.shape[-1] // 256
+    w_first = w_buf.shape[0] - n_groups
     first_depth = N_FIRST * 256
     n_rows = n_batch * tok_dev
     n_steps = tok_dev // MINI_BATCH
@@ -128,7 +129,7 @@
         return pltpu.make_async_copy(w_buf.at[pl.ds(part * sum_slots, sum_slots)], sum_hbm.at[:, :, :, columns(n)], sum_sem.at[part])
 
     def hand_on(g):
-        return pltpu.make_async_remote_copy(w_send, w_buf.at[g], send_sem, recv_sem.at[g],
+        return pltpu.make_async_remote_copy(w_send, w_buf.at[w_first + g], send_sem, recv_sem.at[g],
                                             device_id={"seq": lax.rem(me + 1, n_seq)}, device_id_type=pl.DeviceIdType.MESH)
 
     sum_slots = sum_hbm.shape[0]
@@ -248,7 +249,7 @@
             first_w(g).wait()
             start = jnp.concatenate([init_buf[h] for h in range(HEADS_PER_GROUP)], axis=1)
             for b in range(n_batch):
-                w_buf[g, b] = start
+                w_buf[w_first + g, b] = start
 
         @pl.when((me == 0) & first_time & (g + 1 < n_groups))
         def _():
@@ -266,7 +267,7 @@
         for h in range(HEADS_PER_GROUP):
             eta = jnp.where(head == h, (2.0 / MINI_BATCH) * lr_ref[g * HEADS_PER_GROUP + h], eta)
 
-        w_now[...] = w_buf[g]
+        w_now[...] = w_buf[w_first + g]
 
         if n is None:
             def fill(j):
@@ -281,11 +282,14 @@
                 b, first = j * chunk // tok_dev, j * chunk % tok_dev
                 lhs = jnp.concatenate([kvq_buf[2, i, b, pl.ds(first, chunk), :] for i in range(N_FIRST)], axis=1)
                 part = jnp.dot(lhs, theta_buf[slot, :first_depth, :], preferred_element_type=f32)
+                spare = pl.ds(j * chunk, chunk)
+                even = jnp.dot(x_buf[spare, :depth - first_depth], theta_buf[slot, first_depth:, :], preferred_element_type=f32)
                 rows = n_batch * w_buf.shape[2]
                 at, within = j * chunk // rows, j * chunk % rows // w_buf.shape[2]
 
                 def put():
                     w_buf[lax.rem(n, 2) * sum_slots + at, pl.ds(within, chunk // w_buf.shape[2])] = part.reshape(chunk // w_buf.shape[2], *w_buf.shape[2:])
+                    tile_buf[spare, :] = even.astype(bf16)
                 return put
 
         chain(g, eta, fill)
@@ -465,7 +469,7 @@
             in_specs=[hbm] * 6 + [smem], out_specs=(hbm, hbm),
             scratch_shapes=[pltpu.VMEM((n_rows, width_d), bf16), pltpu.VMEM((3, n_groups, n_batch, tok_dev, 256), bf16),
                             pltpu.VMEM((2, width_d, 256), bf16), pltpu.VMEM((n_rows, 256), bf16), pltpu.VMEM((n_batch, tok_dev, 256), bf16),
-                            pltpu.VMEM((n_groups, n_batch, head_dim, 4 * head_dim), f32),
+                            pltpu.VMEM((n_groups + max(0, 2 * sum_slots - N_FIRST), n_batch, head_dim, 4 * head_dim), f32),
                             pltpu.VMEM((n_batch, head_dim, 4 * head_dim), f32), pltpu.VMEM((n_batch, head_dim, 4 * head_dim), f32),
                             pltpu.VMEM((HEADS_PER_GROUP, head_dim, head_dim), f32),
                             pltpu.SemaphoreType.DMA((2,)), pltpu.SemaphoreType.DMA((2,)), pltpu.SemaphoreType.DMA, pltpu.SemaphoreType.DMA((2,)),

time: 281 us -> 281 us (level)
    pallas_call x1, Pallas kernels: 262 us -> 258 us  [per_device(): pl.pallas_call(functools.partial(fused_kernel, n_seq, n_batch, tok_dev, n...]
    pallas_call x1, Pallas kernels: 18.7 us -> 22.1 us  [per_device(): pl.pallas_call(rest_kernel, out_shape=jax.ShapeDtypeStruct((n_rows, width...]
where the time goes in v11:
time: 281 us
  Pallas kernels  280 us (100%)
    pallas_call x1, Pallas kernels, per_device(): pl.pallas_call(functools.partial(fused_kernel, n_seq, n_batch, tok_dev, n...  258 us
    pallas_call x1, Pallas kernels, per_device(): pl.pallas_call(rest_kernel, out_shape=jax.ShapeDtypeStruct((n_rows, width...  22.1 us

profile of v11, /device:TPU:127, one launch (start us, length us, event | category | flops | bytes accessed | tf_op | source)
XLA Modules:
  0.0 280.6 jit_solution(16788452458603367975)
XLA Ops:
  0.0 258.3 %fused.1 = (bf16[8,256,1280]{2,1,0:T(8,128)(2,1)}, f32[4,8,64,3072]{3,2,1,0:T(8,128)}) custom-call(bf16[2048,3072]{1,0:T(8,128)(2,1)} %bitcast.3, bf16[3072,3072]{1,0:T(8,128)(2,1)} %theta_k_hbm.1, bf16[3072,3072]{1,0:T(8,128)(2,1)} %theta_v_hbm.1, bf16[3072,3072]{1,0:T(8,128)(2,1)} %theta_q_hbm.1, bf16[3072,3072]{1,0:T(8,128)(2,1)} %w_hbm.1, ...), custom_call_target="tpu_custom_call" | custom-call | tf_op jit(solution)/shard_map/fused/pallas_call | solution.py:466
  258.3 22.1 %rest.1 = bf16[2048,3072]{1,0:T(8,128)(2,1)} custom-call(bf16[2048,1280]{1,0:T(8,128)(2,1)} %bitcast.4, bf16[3072,3072]{1,0:T(8,128)(2,1)} %w_hbm.1, f32[4,8,64,3072]{3,2,1,0:T(8,128)} %get-tuple-element.8.sum_hbm), custom_call_target="tpu_custom_call" | custom-call | tf_op jit(solution)/shard_map/rest/pallas_call | solution.py:481

commit v12 on v11

--- a/solution.py
+++ b/solution.py
@@ -10,7 +10,7 @@
 MINI_BATCH = 16
 HEADS_PER_GROUP = 4
 SCHEDULE = ((0, 6, (0, 0, 0, 0, 0)), (1, 5, (0, 0, 0, 0, 0)), (3, 3, (0, 0, 0, 0, 0)), (3, 1, (0, 0, 0, 0, 0)),
-            (4, 0, (0, 3, 3, 3, 3)), (5, 0, (3, 6, 6, 6, 6)), (5, 0, (3, 6, 6, 6, 6)), (5, 0, (3, 6, 6, 7, 7)))
+            (4, 0, (0, 3, 3, 3, 3)), (5, 0, (3, 6, 6, 6, 6)), (5, 0, (3, 6, 6, 6, 6)), (5, 0, (4, 7, 7, 7, 7)))
 N_FIRST = 7
 REST_COLUMNS = 512
 bf16, f32 = jnp.bfloat16, jnp.float32
@@ -204,7 +204,8 @@
             rows = pl.ds(i * (n_rows // 2), n_rows // 2)
             if isinstance(c, int):
                 x_copy(i).wait()
-            part = jnp.dot(x_buf[rows, :], theta_buf[slot], preferred_element_type=f32).astype(bf16)
+            pieces = [pl.ds(i * (n_rows // 2) + p * (n_rows // 4), n_rows // 4) for p in range(2)] if isinstance(c, int) else [rows]
+            part = jnp.concatenate([jnp.dot(x_buf[p, :], theta_buf[slot], preferred_element_type=f32).astype(bf16) for p in pieces], axis=0)
             if group is not None and i == 0:
                 last_results(group)
                 before = tile_at(c - 1)
@@ -268,6 +269,8 @@
             eta = jnp.where(head == h, (2.0 / MINI_BATCH) * lr_ref[g * HEADS_PER_GROUP + h], eta)
 
         w_now[...] = w_buf[w_first + g]
+        if n is not None:
+            theta_buf[slot, first_depth:, :] = jnp.zeros((depth - first_depth, 256), bf16)
 
         if n is None:
             def fill(j):
@@ -281,30 +284,28 @@
             def fill(j):
                 b, first = j * chunk // tok_dev, j * chunk % tok_dev
                 lhs = jnp.concatenate([kvq_buf[2, i, b, pl.ds(first, chunk), :] for i in range(N_FIRST)], axis=1)
-                part = jnp.dot(lhs, theta_buf[slot, :first_depth, :], preferred_element_type=f32)
-                spare = pl.ds(j * chunk, chunk)
-                even = jnp.dot(x_buf[spare, :depth - first_depth], theta_buf[slot, first_depth:, :], preferred_element_type=f32)
+                lhs = jnp.concatenate([lhs, x_buf[pl.ds(j * chunk, chunk), :depth - first_depth]], axis=1)
+                part = jnp.dot(lhs, theta_buf[slot], preferred_element_type=f32)
                 rows = n_batch * w_buf.shape[2]
                 at, within = j * chunk // rows, j * chunk % rows // w_buf.shape[2]
 
                 def put():
                     w_buf[lax.rem(n, 2) * sum_slots + at, pl.ds(within, chunk // w_buf.shape[2])] = part.reshape(chunk // w_buf.shape[2], *w_buf.shape[2:])
-                    tile_buf[spare, :] = even.astype(bf16)
                 return put
 
         chain(g, eta, fill)
+
+        @pl.when((me < n_seq - 1) & first_time & (g > 0))
+        def _():
+            hand_on(0).wait_send()
+
+        @pl.when((me < n_seq - 1) & first_time)
+        def _():
+            w_send[...] = w_now[...]
+            hand_on(g).start()
 
         if n is not None:
             sum_copy(n).start()
-
-        @pl.when((me < n_seq - 1) & first_time & (g > 0))
-        def _():
-            hand_on(0).wait_send()
-
-        @pl.when((me < n_seq - 1) & first_time)
-        def _():
-            w_send[...] = w_now[...]
-            hand_on(g).start()
 
     def last_results(g):
         for units in (pl.ds(0, half), pl.ds(half, half)):
@@ -399,54 +400,62 @@
         return pltpu.make_async_copy(o_hbm.at[rows], o_buf.at[rows], o_sem.at[i])
 
     def w_copy(n):
-        slot = lax.rem(n, 2)
+        slot = lax.rem(n, 3)
         return pltpu.make_async_copy(w_hbm.at[pl.ds(w_hbm.shape[0] - depth, depth), columns(n)], w_buf.at[slot], w_sem.at[slot])
 
     def sum_copy(n, i):
-        slot, part = lax.rem(n, 2), pl.ds(i * slots, slots)
+        slot, part = lax.rem(n, 3), pl.ds(i * slots, slots)
         return pltpu.make_async_copy(sum_hbm.at[part, :, :, columns(n)], sum_buf.at[slot, part], sum_sem.at[slot, i])
 
     def out_copy(n, i):
         slot, rows = lax.rem(n, 2), pl.ds(i * half, half)
         return pltpu.make_async_copy(out_buf.at[slot, rows], out_hbm.at[rows, columns(n)], out_sem.at[slot, i])
+
+    def start(n):
+        w_copy(n).start()
+        for i in range(2):
+            sum_copy(n, i).start()
+
+    def product(n, i):
+        rows = pl.ds(i * half, half)
+        so_far = sum_buf[lax.rem(n, 3), pl.ds(i * slots, slots)].reshape(half, REST_COLUMNS)
+        part = jnp.dot(o_buf[rows, :], w_buf[lax.rem(n, 3)], preferred_element_type=f32)
+        out_buf[lax.rem(n, 2), rows, :] = (part + so_far).astype(bf16)
 
     first = jnp.int32(0)
     w_copy(first).start()
     for i in range(2):
         o_copy(i).start()
         sum_copy(first, i).start()
-    w_copy(first + 1).start()
+    start(first + 1)
+    w_copy(first).wait()
+    for i in range(2):
+        o_copy(i).wait()
+        sum_copy(first, i).wait()
+        product(first, i)
+        out_copy(first, i).start()
 
     def part(n, _):
-        slot = lax.rem(n, 2)
+        @pl.when((n >= 2) & (n + 1 < n_parts))
+        def _():
+            start(n + 1)
+
+        @pl.when(n >= 2)
+        def _():
+            for i in range(2):
+                out_copy(n - 2, i).wait()
+
         w_copy(n).wait()
-
-        @pl.when(n + 1 < n_parts)
-        def _():
-            for i in range(2):
-                sum_copy(n + 1, i).start()
-
-        for i in range(2):
-            @pl.when(n == 0)
-            def _():
-                o_copy(i).wait()
-
-            @pl.when(n >= 2)
-            def _():
-                out_copy(n - 2, i).wait()
-
+        for i in range(2):
             sum_copy(n, i).wait()
-            rows = pl.ds(i * half, half)
-            so_far = sum_buf[slot, pl.ds(i * slots, slots)].reshape(half, REST_COLUMNS)
-            out_buf[slot, rows, :] = (jnp.dot(o_buf[rows, :], w_buf[slot], preferred_element_type=f32) + so_far).astype(bf16)
+        for i in range(2):
+            product(n, i)
+        for i in range(2):
             out_copy(n, i).start()
-
-        @pl.when(n + 2 < n_parts)
-        def _():
-            w_copy(n + 2).start()
         return 0
 
-    lax.fori_loop(0, n_parts, part, 0)
+    start(first + 2)
+    lax.fori_loop(1, n_parts, part, 0)
     for n in range(n_parts - 2, n_parts):
         for i in range(2):
             out_copy(n, i).wait()
@@ -482,9 +491,9 @@
             rest_kernel,
             out_shape=jax.ShapeDtypeStruct((n_rows, width_d), bf16),
             in_specs=[hbm] * 3, out_specs=hbm,
-            scratch_shapes=[pltpu.VMEM((n_rows, depth), bf16), pltpu.VMEM((2, depth, REST_COLUMNS), bf16),
-                            pltpu.VMEM((2, sum_slots, n_batch, head_dim, REST_COLUMNS), f32), pltpu.VMEM((2, n_rows, REST_COLUMNS), bf16),
-                            pltpu.SemaphoreType.DMA((2,)), pltpu.SemaphoreType.DMA((2,)), pltpu.SemaphoreType.DMA((2, 2)), pltpu.SemaphoreType.DMA((2, 2))],
+            scratch_shapes=[pltpu.VMEM((n_rows, depth), bf16), pltpu.VMEM((3, depth, REST_COLUMNS), bf16),
+                            pltpu.VMEM((3, sum_slots, n_batch, head_dim, REST_COLUMNS), f32), pltpu.VMEM((2, n_rows, REST_COLUMNS), bf16),
+                            pltpu.SemaphoreType.DMA((2,)), pltpu.SemaphoreType.DMA((3,)), pltpu.SemaphoreType.DMA((3, 2)), pltpu.SemaphoreType.DMA((2, 2))],
             compiler_params=pltpu.CompilerParams(vmem_limit_bytes=67043328),
             name="rest",
         )(o.reshape(n_rows, depth), w_out, first_sum)

time: 281 us -> 273 us (0.972)
  Pallas kernels: 280 us -> 273 us
    pallas_call x1, Pallas kernels: 258 us -> 250 us  [per_device(): pl.pallas_call(functools.partial(fused_kernel, n_seq, n_batch, tok_dev, n...]
where the time goes in v12:
time: 273 us
  Pallas kernels  273 us (100%)
    pallas_call x1, Pallas kernels, per_device(): pl.pallas_call(functools.partial(fused_kernel, n_seq, n_batch, tok_dev, n...  250 us
    pallas_call x1, Pallas kernels, per_device(): pl.pallas_call(rest_kernel, out_shape=jax.ShapeDtypeStruct((n_rows, width...  23.3 us

profile of v12, /device:TPU:127, one launch (start us, length us, event | category | flops | bytes accessed | tf_op | source)
XLA Modules:
  0.0 273.1 jit_solution(7962486466440602462)
XLA Ops:
  0.0 249.7 %fused.1 = (bf16[8,256,1280]{2,1,0:T(8,128)(2,1)}, f32[4,8,64,3072]{3,2,1,0:T(8,128)}) custom-call(bf16[2048,3072]{1,0:T(8,128)(2,1)} %bitcast.3, bf16[3072,3072]{1,0:T(8,128)(2,1)} %theta_k_hbm.1, bf16[3072,3072]{1,0:T(8,128)(2,1)} %theta_v_hbm.1, bf16[3072,3072]{1,0:T(8,128)(2,1)} %theta_q_hbm.1, bf16[3072,3072]{1,0:T(8,128)(2,1)} %w_hbm.1, ...), custom_call_target="tpu_custom_call" | custom-call | tf_op jit(solution)/shard_map/fused/pallas_call | solution.py:475
  249.7 23.3 %rest.1 = bf16[2048,3072]{1,0:T(8,128)(2,1)} custom-call(bf16[2048,1280]{1,0:T(8,128)(2,1)} %bitcast.4, bf16[3072,3072]{1,0:T(8,128)(2,1)} %w_hbm.1, f32[4,8,64,3072]{3,2,1,0:T(8,128)} %get-tuple-element.8.sum_hbm), custom_call_target="tpu_custom_call" | custom-call | tf_op jit(solution)/shard_map/rest/pallas_call | solution.py:490

commit v13 on v12

--- a/solution.py
+++ b/solution.py
@@ -9,8 +9,8 @@
 
 MINI_BATCH = 16
 HEADS_PER_GROUP = 4
-SCHEDULE = ((0, 6, (0, 0, 0, 0, 0)), (1, 5, (0, 0, 0, 0, 0)), (3, 3, (0, 0, 0, 0, 0)), (3, 1, (0, 0, 0, 0, 0)),
-            (4, 0, (0, 3, 3, 3, 3)), (5, 0, (3, 6, 6, 6, 6)), (5, 0, (3, 6, 6, 6, 6)), (5, 0, (4, 7, 7, 7, 7)))
+SCHEDULE = ((0, 7, (0, 0, 0, 0, 0)), (1, 6, (0, 0, 0, 0, 0)), (3, 4, (0, 0, 0, 0, 0)), (3, 1, (0, 0, 0, 0, 0)),
+            (4, 0, (0, 3, 3, 3, 3)), (4, 0, (0, 3, 3, 3, 3)), (5, 0, (3, 6, 6, 6, 6)), (5, 0, (4, 7, 7, 7, 7)))
 N_FIRST = 7
 REST_COLUMNS = 512
 bf16, f32 = jnp.bfloat16, jnp.float32
@@ -159,12 +159,12 @@
     def tokens(kind, g, units, j):
         return kvq_buf[kind, g, units, pl.ds(j * MINI_BATCH, MINI_BATCH), :]
 
-    def chain_step(g, eta, j, now, before):
+    def chain_step(g, eta, j, now, before, w_start=None):
         k_rows = z = None
         if now is not None:
             k_rows = per_head_rows(tokens(0, g, now, j)) if j < n_steps else []
             rows = k_rows + (per_head_rows(tokens(2, g, now, j - 1)) if j > 0 else [])
-            lhs, rhs = times_w(rows, w_now[now])
+            lhs, rhs = times_w(rows, w_now[now] if w_start is None or j > 0 else w_start[now])
         if before is not None:
             units, step, keys, inputs = before
             r = (inputs - tokens(1, g, units, step).astype(f32)) * eta
@@ -182,16 +182,16 @@
             if j > 0:
                 o_buf[now, pl.ds((j - 1) * MINI_BATCH, MINI_BATCH), :] = own_columns(prod, 4 * MINI_BATCH if j < n_steps else 0).astype(bf16)
         if before is not None:
-            w_now[units] = w_now[units] - jnp.stack(change)
+            w_now[units] = (w_now[units] if w_start is None or step > 0 else w_start[units]) - jnp.stack(change)
         return k_rows, z
 
-    def chain(g, eta, fill):
+    def chain(g, eta, fill, w_start=None):
         one, two = pl.ds(0, half), pl.ds(half, half)
         open_two = None
         for j in range(n_steps):
             put = fill(j)
-            open_one = (one, j, *chain_step(g, eta, j, one, open_two))
-            open_two = (two, j, *chain_step(g, eta, j, two, open_one))
+            open_one = (one, j, *chain_step(g, eta, j, one, open_two, w_start))
+            open_two = (two, j, *chain_step(g, eta, j, two, open_one, w_start))
             put()
         chain_step(g, eta, n_steps, None, open_two)
 
@@ -268,8 +268,8 @@
         for h in range(HEADS_PER_GROUP):
             eta = jnp.where(head == h, (2.0 / MINI_BATCH) * lr_ref[g * HEADS_PER_GROUP + h], eta)
 
-        w_now[...] = w_buf[w_first + g]
         if n is not None:
+            w_now[...] = w_buf[w_first + g]
             theta_buf[slot, first_depth:, :] = jnp.zeros((depth - first_depth, 256), bf16)
 
         if n is None:
@@ -293,7 +293,7 @@
                     w_buf[lax.rem(n, 2) * sum_slots + at, pl.ds(within, chunk // w_buf.shape[2])] = part.reshape(chunk // w_buf.shape[2], *w_buf.shape[2:])
                 return put
 
-        chain(g, eta, fill)
+        chain(g, eta, fill, w_buf.at[w_first + g] if n is None else None)
 
         @pl.when((me < n_seq - 1) & first_time & (g > 0))
         def _():
@@ -427,11 +427,12 @@
     for i in range(2):
         o_copy(i).start()
         sum_copy(first, i).start()
-    start(first + 1)
     w_copy(first).wait()
     for i in range(2):
         o_copy(i).wait()
         sum_copy(first, i).wait()
+        if i == 1:
+            start(first + 1)
         product(first, i)
         out_copy(first, i).start()
 

time: 273 us -> 273 us (level)
  no operation moved by 1% of the time
where the time goes in v13:
time: 273 us
  Pallas kernels  273 us (100%)
    pallas_call x1, Pallas kernels, per_device(): pl.pallas_call(functools.partial(fused_kernel, n_seq, n_batch, tok_dev, n...  249 us
    pallas_call x1, Pallas kernels, per_device(): pl.pallas_call(rest_kernel, out_shape=jax.ShapeDtypeStruct((n_rows, width...  24.4 us

profile of v13, /device:TPU:127, one launch (start us, length us, event | category | flops | bytes accessed | tf_op | source)
XLA Modules:
  0.0 273.4 jit_solution(14676097280951857632)
XLA Ops:
  0.0 248.8 %fused.1 = (bf16[8,256,1280]{2,1,0:T(8,128)(2,1)}, f32[4,8,64,3072]{3,2,1,0:T(8,128)}) custom-call(bf16[2048,3072]{1,0:T(8,128)(2,1)} %bitcast.3, bf16[3072,3072]{1,0:T(8,128)(2,1)} %theta_k_hbm.1, bf16[3072,3072]{1,0:T(8,128)(2,1)} %theta_v_hbm.1, bf16[3072,3072]{1,0:T(8,128)(2,1)} %theta_q_hbm.1, bf16[3072,3072]{1,0:T(8,128)(2,1)} %w_hbm.1, ...), custom_call_target="tpu_custom_call" | custom-call | tf_op jit(solution)/shard_map/fused/pallas_call | solution.py:476
  248.8 24.4 %rest.1 = bf16[2048,3072]{1,0:T(8,128)(2,1)} custom-call(bf16[2048,1280]{1,0:T(8,128)(2,1)} %bitcast.4, bf16[3072,3072]{1,0:T(8,128)(2,1)} %w_hbm.1, f32[4,8,64,3072]{3,2,1,0:T(8,128)} %get-tuple-element.8.sum_hbm), custom_call_target="tpu_custom_call" | custom-call | tf_op jit(solution)/shard_map/rest/pallas_call | solution.py:491

commit v14 on v13

--- a/solution.py
+++ b/solution.py
@@ -389,76 +389,84 @@
 
 def rest_kernel(o_hbm, w_hbm, sum_hbm, out_hbm, o_buf, w_buf, sum_buf, out_buf, o_sem, w_sem, sum_sem, out_sem):
     n_rows, depth = o_buf.shape
-    half, slots = n_rows // 2, sum_buf.shape[1] // 2
+    pieces = sum_buf.shape[1]
+    piece, half = n_rows // pieces, n_rows // 2
     n_parts = out_hbm.shape[1] // REST_COLUMNS
 
     def columns(n):
         return pl.ds(pl.multiple_of(n * REST_COLUMNS, REST_COLUMNS), REST_COLUMNS)
 
     def o_copy(i):
-        rows = pl.ds(i * half, half)
+        rows = pl.ds(i * piece, piece)
         return pltpu.make_async_copy(o_hbm.at[rows], o_buf.at[rows], o_sem.at[i])
 
-    def w_copy(n):
+    def w_copy(n, i):
+        slot, rows = lax.rem(n, 3), depth // 2
+        return pltpu.make_async_copy(w_hbm.at[pl.ds(w_hbm.shape[0] - depth + i * rows, rows), columns(n)],
+                                     w_buf.at[slot, pl.ds(i * rows, rows)], w_sem.at[slot, i])
+
+    def sum_copy(n, i):
         slot = lax.rem(n, 3)
-        return pltpu.make_async_copy(w_hbm.at[pl.ds(w_hbm.shape[0] - depth, depth), columns(n)], w_buf.at[slot], w_sem.at[slot])
-
-    def sum_copy(n, i):
-        slot, part = lax.rem(n, 3), pl.ds(i * slots, slots)
-        return pltpu.make_async_copy(sum_hbm.at[part, :, :, columns(n)], sum_buf.at[slot, part], sum_sem.at[slot, i])
+        return pltpu.make_async_copy(sum_hbm.at[i, :, :, columns(n)], sum_buf.at[slot, i], sum_sem.at[slot, i])
 
     def out_copy(n, i):
-        slot, rows = lax.rem(n, 2), pl.ds(i * half, half)
+        slot, rows = lax.rem(n, 2), pl.ds(i * piece, piece)
         return pltpu.make_async_copy(out_buf.at[slot, rows], out_hbm.at[rows, columns(n)], out_sem.at[slot, i])
 
     def start(n):
-        w_copy(n).start()
         for i in range(2):
+            w_copy(n, i).start()
+        for i in range(pieces):
             sum_copy(n, i).start()
 
     def product(n, i):
         rows = pl.ds(i * half, half)
-        so_far = sum_buf[lax.rem(n, 3), pl.ds(i * slots, slots)].reshape(half, REST_COLUMNS)
+        so_far = sum_buf[lax.rem(n, 3), pl.ds(i * (pieces // 2), pieces // 2)].reshape(half, REST_COLUMNS)
         part = jnp.dot(o_buf[rows, :], w_buf[lax.rem(n, 3)], preferred_element_type=f32)
         out_buf[lax.rem(n, 2), rows, :] = (part + so_far).astype(bf16)
 
     first = jnp.int32(0)
-    w_copy(first).start()
     for i in range(2):
+        w_copy(first, i).start()
+    for i in range(pieces):
         o_copy(i).start()
         sum_copy(first, i).start()
-    w_copy(first).wait()
     for i in range(2):
+        w_copy(first, i).wait()
+    for i in range(pieces):
         o_copy(i).wait()
         sum_copy(first, i).wait()
-        if i == 1:
+        if i == pieces // 2 - 1:
             start(first + 1)
-        product(first, i)
+            product(first, 0)
+    start(first + 2)
+    product(first, 1)
+    for i in range(pieces):
         out_copy(first, i).start()
 
     def part(n, _):
-        @pl.when((n >= 2) & (n + 1 < n_parts))
-        def _():
-            start(n + 1)
+        @pl.when(n + 2 < n_parts)
+        def _():
+            start(n + 2)
 
         @pl.when(n >= 2)
         def _():
-            for i in range(2):
+            for i in range(pieces):
                 out_copy(n - 2, i).wait()
 
-        w_copy(n).wait()
         for i in range(2):
+            w_copy(n, i).wait()
+        for i in range(pieces):
             sum_copy(n, i).wait()
         for i in range(2):
             product(n, i)
-        for i in range(2):
+        for i in range(pieces):
             out_copy(n, i).start()
         return 0
 
-    start(first + 2)
     lax.fori_loop(1, n_parts, part, 0)
     for n in range(n_parts - 2, n_parts):
-        for i in range(2):
+        for i in range(pieces):
             out_copy(n, i).wait()
 
 
@@ -494,7 +502,7 @@
             in_specs=[hbm] * 3, out_specs=hbm,
             scratch_shapes=[pltpu.VMEM((n_rows, depth), bf16), pltpu.VMEM((3, depth, REST_COLUMNS), bf16),
                             pltpu.VMEM((3, sum_slots, n_batch, head_dim, REST_COLUMNS), f32), pltpu.VMEM((2, n_rows, REST_COLUMNS), bf16),
-                            pltpu.SemaphoreType.DMA((2,)), pltpu.SemaphoreType.DMA((3,)), pltpu.SemaphoreType.DMA((3, 2)), pltpu.SemaphoreType.DMA((2, 2))],
+                            pltpu.SemaphoreType.DMA((sum_slots,)), pltpu.SemaphoreType.DMA((3, 2)), pltpu.SemaphoreType.DMA((3, sum_slots)), pltpu.SemaphoreType.DMA((2, sum_slots))],
             compiler_params=pltpu.CompilerParams(vmem_limit_bytes=67043328),
             name="rest",
         )(o.reshape(n_rows, depth), w_out, first_sum)

time: 273 us -> 272 us (level)
  no operation moved by 1% of the time
where the time goes in v14:
time: 272 us; the launch traced here: 271 us
  Pallas kernels  271 us (100%)
    pallas_call x1, Pallas kernels, per_device(): pl.pallas_call(functools.partial(fused_kernel, n_seq, n_batch, tok_dev, n...  249 us
    pallas_call x1, Pallas kernels, per_device(): pl.pallas_call(rest_kernel, out_shape=jax.ShapeDtypeStruct((n_rows, width...  22.5 us

profile of v14, /device:TPU:127, one launch (start us, length us, event | category | flops | bytes accessed | tf_op | source)
XLA Modules:
  0.0 271.5 jit_solution(137810993362434080)
XLA Ops:
  0.0 248.8 %fused.1 = (bf16[8,256,1280]{2,1,0:T(8,128)(2,1)}, f32[4,8,64,3072]{3,2,1,0:T(8,128)}) custom-call(bf16[2048,3072]{1,0:T(8,128)(2,1)} %bitcast.3, bf16[3072,3072]{1,0:T(8,128)(2,1)} %theta_k_hbm.1, bf16[3072,3072]{1,0:T(8,128)(2,1)} %theta_v_hbm.1, bf16[3072,3072]{1,0:T(8,128)(2,1)} %theta_q_hbm.1, bf16[3072,3072]{1,0:T(8,128)(2,1)} %w_hbm.1, ...), custom_call_target="tpu_custom_call" | custom-call | tf_op jit(solution)/shard_map/fused/pallas_call | solution.py:484
  248.8 22.5 %rest.1 = bf16[2048,3072]{1,0:T(8,128)(2,1)} custom-call(bf16[2048,1280]{1,0:T(8,128)(2,1)} %bitcast.4, bf16[3072,3072]{1,0:T(8,128)(2,1)} %w_hbm.1, f32[4,8,64,3072]{3,2,1,0:T(8,128)} %get-tuple-element.8.sum_hbm), custom_call_target="tpu_custom_call" | custom-call | tf_op jit(solution)/shard_map/rest/pallas_call | solution.py:499

commit v15 on v14

--- a/solution.py
+++ b/solution.py
@@ -428,19 +428,23 @@
     first = jnp.int32(0)
     for i in range(2):
         w_copy(first, i).start()
-    for i in range(pieces):
+    for i in range(pieces // 2):
         o_copy(i).start()
         sum_copy(first, i).start()
     for i in range(2):
         w_copy(first, i).wait()
-    for i in range(pieces):
-        o_copy(i).wait()
-        sum_copy(first, i).wait()
-        if i == pieces // 2 - 1:
+    for h in range(2):
+        for i in range(h * pieces // 2, (h + 1) * pieces // 2):
+            o_copy(i).wait()
+            sum_copy(first, i).wait()
+        if h == 0:
+            for i in range(pieces // 2, pieces):
+                o_copy(i).start()
+                sum_copy(first, i).start()
+        else:
             start(first + 1)
-            product(first, 0)
+        product(first, h)
     start(first + 2)
-    product(first, 1)
     for i in range(pieces):
         out_copy(first, i).start()
 

time: 272 us -> 273 us (level)
  no operation moved by 1% of the time
where the time goes in v15:
time: 273 us
  Pallas kernels  273 us (100%)
    pallas_call x1, Pallas kernels, per_device(): pl.pallas_call(functools.partial(fused_kernel, n_seq, n_batch, tok_dev, n...  249 us
    pallas_call x1, Pallas kernels, per_device(): pl.pallas_call(rest_kernel, out_shape=jax.ShapeDtypeStruct((n_rows, width...  24.1 us

profile of v15, /device:TPU:127, one launch (start us, length us, event | category | flops | bytes accessed | tf_op | source)
XLA Modules:
  0.0 273.1 jit_solution(17535440332806184841)
XLA Ops:
  0.0 248.8 %fused.1 = (bf16[8,256,1280]{2,1,0:T(8,128)(2,1)}, f32[4,8,64,3072]{3,2,1,0:T(8,128)}) custom-call(bf16[2048,3072]{1,0:T(8,128)(2,1)} %bitcast.3, bf16[3072,3072]{1,0:T(8,128)(2,1)} %theta_k_hbm.1, bf16[3072,3072]{1,0:T(8,128)(2,1)} %theta_v_hbm.1, bf16[3072,3072]{1,0:T(8,128)(2,1)} %theta_q_hbm.1, bf16[3072,3072]{1,0:T(8,128)(2,1)} %w_hbm.1, ...), custom_call_target="tpu_custom_call" | custom-call | tf_op jit(solution)/shard_map/fused/pallas_call | solution.py:488
  248.8 24.1 %rest.1 = bf16[2048,3072]{1,0:T(8,128)(2,1)} custom-call(bf16[2048,1280]{1,0:T(8,128)(2,1)} %bitcast.4, bf16[3072,3072]{1,0:T(8,128)(2,1)} %w_hbm.1, f32[4,8,64,3072]{3,2,1,0:T(8,128)} %get-tuple-element.8.sum_hbm), custom_call_target="tpu_custom_call" | custom-call | tf_op jit(solution)/shard_map/rest/pallas_call | solution.py:503

commit v16 on v15

--- a/solution.py
+++ b/solution.py
@@ -84,7 +84,7 @@
         return n
 
     n_tiles = 3 * n_groups
-    n_out_tiles = sum_hbm.shape[-1] // 256
+    n_out_tiles = sum_hbm.shape[0]
     w_first = w_buf.shape[0] - n_groups
     first_depth = N_FIRST * 256
     n_rows = n_batch * tok_dev
@@ -126,13 +126,13 @@
 
     def sum_copy(n):
         part = lax.rem(n, 2)
-        return pltpu.make_async_copy(w_buf.at[pl.ds(part * sum_slots, sum_slots)], sum_hbm.at[:, :, :, columns(n)], sum_sem.at[part])
+        return pltpu.make_async_copy(w_buf.at[pl.ds(part * sum_slots, sum_slots)], sum_hbm.at[n], sum_sem.at[part])
 
     def hand_on(g):
         return pltpu.make_async_remote_copy(w_send, w_buf.at[w_first + g], send_sem, recv_sem.at[g],
                                             device_id={"seq": lax.rem(me + 1, n_seq)}, device_id_type=pl.DeviceIdType.MESH)
 
-    sum_slots = sum_hbm.shape[0]
+    sum_slots = sum_hbm.shape[1]
 
     def first_w(g):
         return pltpu.make_async_copy(w_init_hbm.at[pl.ds(g * HEADS_PER_GROUP, HEADS_PER_GROUP)], init_buf, init_sem)
@@ -389,7 +389,7 @@
 
 def rest_kernel(o_hbm, w_hbm, sum_hbm, out_hbm, o_buf, w_buf, sum_buf, out_buf, o_sem, w_sem, sum_sem, out_sem):
     n_rows, depth = o_buf.shape
-    pieces = sum_buf.shape[1]
+    per_part, pieces = sum_buf.shape[1:3]
     piece, half = n_rows // pieces, n_rows // 2
     n_parts = out_hbm.shape[1] // REST_COLUMNS
 
@@ -406,8 +406,8 @@
                                      w_buf.at[slot, pl.ds(i * rows, rows)], w_sem.at[slot, i])
 
     def sum_copy(n, i):
-        slot = lax.rem(n, 3)
-        return pltpu.make_async_copy(sum_hbm.at[i, :, :, columns(n)], sum_buf.at[slot, i], sum_sem.at[slot, i])
+        slot, at = lax.rem(n, 3), pl.ds(i % 2 * (pieces // 2), pieces // 2)
+        return pltpu.make_async_copy(sum_hbm.at[n * per_part + i // 2, at], sum_buf.at[slot, i // 2, at], sum_sem.at[slot, i])
 
     def out_copy(n, i):
         slot, rows = lax.rem(n, 2), pl.ds(i * piece, piece)
@@ -416,35 +416,33 @@
     def start(n):
         for i in range(2):
             w_copy(n, i).start()
-        for i in range(pieces):
+        for i in range(2 * per_part):
             sum_copy(n, i).start()
 
     def product(n, i):
         rows = pl.ds(i * half, half)
-        so_far = sum_buf[lax.rem(n, 3), pl.ds(i * (pieces // 2), pieces // 2)].reshape(half, REST_COLUMNS)
+        so_far = jnp.concatenate([sum_buf[lax.rem(n, 3), p, pl.ds(i * (pieces // 2), pieces // 2)].reshape(half, 256) for p in range(per_part)], axis=1)
         part = jnp.dot(o_buf[rows, :], w_buf[lax.rem(n, 3)], preferred_element_type=f32)
         out_buf[lax.rem(n, 2), rows, :] = (part + so_far).astype(bf16)
 
     first = jnp.int32(0)
     for i in range(2):
         w_copy(first, i).start()
-    for i in range(pieces // 2):
+    for i in range(pieces):
         o_copy(i).start()
+    for i in range(2 * per_part):
         sum_copy(first, i).start()
     for i in range(2):
         w_copy(first, i).wait()
+    start(first + 1)
     for h in range(2):
         for i in range(h * pieces // 2, (h + 1) * pieces // 2):
             o_copy(i).wait()
+        for i in range(h, 2 * per_part, 2):
             sum_copy(first, i).wait()
+        product(first, h)
         if h == 0:
-            for i in range(pieces // 2, pieces):
-                o_copy(i).start()
-                sum_copy(first, i).start()
-        else:
-            start(first + 1)
-        product(first, h)
-    start(first + 2)
+            start(first + 2)
     for i in range(pieces):
         out_copy(first, i).start()
 
@@ -460,7 +458,7 @@
 
         for i in range(2):
             w_copy(n, i).wait()
-        for i in range(pieces):
+        for i in range(2 * per_part):
             sum_copy(n, i).wait()
         for i in range(2):
             product(n, i)
@@ -487,7 +485,7 @@
         sum_slots = n_rows // (n_batch * head_dim)
         o, first_sum = pl.pallas_call(
             functools.partial(fused_kernel, n_seq, n_batch, tok_dev, n_groups),
-            out_shape=(jax.ShapeDtypeStruct((n_batch, tok_dev, width - 256 * N_FIRST), bf16), jax.ShapeDtypeStruct((sum_slots, n_batch, head_dim, width_d), f32)),
+            out_shape=(jax.ShapeDtypeStruct((n_batch, tok_dev, width - 256 * N_FIRST), bf16), jax.ShapeDtypeStruct((width_d // 256, sum_slots, n_batch, head_dim, 256), f32)),
             in_specs=[hbm] * 6 + [smem], out_specs=(hbm, hbm),
             scratch_shapes=[pltpu.VMEM((n_rows, width_d), bf16), pltpu.VMEM((3, n_groups, n_batch, tok_dev, 256), bf16),
                             pltpu.VMEM((2, width_d, 256), bf16), pltpu.VMEM((n_rows, 256), bf16), pltpu.VMEM((n_batch, tok_dev, 256), bf16),
@@ -505,8 +503,8 @@
             out_shape=jax.ShapeDtypeStruct((n_rows, width_d), bf16),
             in_specs=[hbm] * 3, out_specs=hbm,
             scratch_shapes=[pltpu.VMEM((n_rows, depth), bf16), pltpu.VMEM((3, depth, REST_COLUMNS), bf16),
-                            pltpu.VMEM((3, sum_slots, n_batch, head_dim, REST_COLUMNS), f32), pltpu.VMEM((2, n_rows, REST_COLUMNS), bf16),
-                            pltpu.SemaphoreType.DMA((sum_slots,)), pltpu.SemaphoreType.DMA((3, 2)), pltpu.SemaphoreType.DMA((3, sum_slots)), pltpu.SemaphoreType.DMA((2, sum_slots))],
+                            pltpu.VMEM((3, REST_COLUMNS // 256, sum_slots, n_batch, head_dim, 256), f32), pltpu.VMEM((2, n_rows, REST_COLUMNS), bf16),
+                            pltpu.SemaphoreType.DMA((sum_slots,)), pltpu.SemaphoreType.DMA((3, 2)), pltpu.SemaphoreType.DMA((3, 2 * REST_COLUMNS // 256)), pltpu.SemaphoreType.DMA((2, sum_slots))],
             compiler_params=pltpu.CompilerParams(vmem_limit_bytes=67043328),
             name="rest",
         )(o.reshape(n_rows, depth), w_out, first_sum)

time: 273 us -> 271 us (level)
  no operation moved by 1% of the time
where the time goes in v16:
time: 271 us
  Pallas kernels  271 us (100%)
    pallas_call x1, Pallas kernels, per_device(): pl.pallas_call(functools.partial(fused_kernel, n_seq, n_batch, tok_dev, n...  249 us
    pallas_call x1, Pallas kernels, per_device(): pl.pallas_call(rest_kernel, out_shape=jax.ShapeDtypeStruct((n_rows, width...  22.5 us

profile of v16, /device:TPU:127, one launch (start us, length us, event | category | flops | bytes accessed | tf_op | source)
XLA Modules:
  0.0 271.2 jit_solution(16966604818361330730)
XLA Ops:
  0.0 248.5 %fused.1 = (bf16[8,256,1280]{2,1,0:T(8,128)(2,1)}, f32[12,4,8,64,256]{4,3,2,1,0:T(8,128)}) custom-call(bf16[2048,3072]{1,0:T(8,128)(2,1)} %bitcast.3, bf16[3072,3072]{1,0:T(8,128)(2,1)} %theta_k_hbm.1, bf16[3072,3072]{1,0:T(8,128)(2,1)} %theta_v_hbm.1, bf16[3072,3072]{1,0:T(8,128)(2,1)} %theta_q_hbm.1, bf16[3072,3072]{1,0:T(8,128)(2,1)} %w_hbm.1, ...), custom_call_target="tpu_custom_call" | custom-call | tf_op jit(solution)/shard_map/fused/pallas_call | solution.py:486
  248.5 22.5 %rest.1 = bf16[2048,3072]{1,0:T(8,128)(2,1)} custom-call(bf16[2048,1280]{1,0:T(8,128)(2,1)} %bitcast.4, bf16[3072,3072]{1,0:T(8,128)(2,1)} %w_hbm.1, f32[12,4,8,64,256]{4,3,2,1,0:T(8,128)} %get-tuple-element.8.sum_hbm), custom_call_target="tpu_custom_call" | custom-call | tf_op jit(solution)/shard_map/rest/pallas_call | solution.py:501

commit v17 on v16

--- a/solution.py
+++ b/solution.py
@@ -428,21 +428,28 @@
     first = jnp.int32(0)
     for i in range(2):
         w_copy(first, i).start()
-    for i in range(pieces):
-        o_copy(i).start()
-    for i in range(2 * per_part):
-        sum_copy(first, i).start()
-    for i in range(2):
-        w_copy(first, i).wait()
-    start(first + 1)
-    for h in range(2):
+    def start_half(h):
+        for i in range(h * pieces // 2, (h + 1) * pieces // 2):
+            o_copy(i).start()
+        for i in range(h, 2 * per_part, 2):
+            sum_copy(first, i).start()
+
+    def wait_half(h):
         for i in range(h * pieces // 2, (h + 1) * pieces // 2):
             o_copy(i).wait()
         for i in range(h, 2 * per_part, 2):
             sum_copy(first, i).wait()
-        product(first, h)
-        if h == 0:
-            start(first + 2)
+
+    start_half(0)
+    for i in range(2):
+        w_copy(first, i).wait()
+    start_half(1)
+    wait_half(0)
+    start(first + 1)
+    product(first, 0)
+    wait_half(1)
+    start(first + 2)
+    product(first, 1)
     for i in range(pieces):
         out_copy(first, i).start()
 

time: 271 us -> 271 us (level)
  no operation moved by 1% of the time
where the time goes in v17:
time: 271 us
  Pallas kernels  271 us (100%)
    pallas_call x1, Pallas kernels, per_device(): pl.pallas_call(functools.partial(fused_kernel, n_seq, n_batch, tok_dev, n...  249 us
    pallas_call x1, Pallas kernels, per_device(): pl.pallas_call(rest_kernel, out_shape=jax.ShapeDtypeStruct((n_rows, width...  22.1 us

profile of v17, /device:TPU:127, one launch (start us, length us, event | category | flops | bytes accessed | tf_op | source)
XLA Modules:
  0.0 270.8 jit_solution(18213032568687975369)
XLA Ops:
  0.0 248.5 %fused.1 = (bf16[8,256,1280]{2,1,0:T(8,128)(2,1)}, f32[12,4,8,64,256]{4,3,2,1,0:T(8,128)}) custom-call(bf16[2048,3072]{1,0:T(8,128)(2,1)} %bitcast.3, bf16[3072,3072]{1,0:T(8,128)(2,1)} %theta_k_hbm.1, bf16[3072,3072]{1,0:T(8,128)(2,1)} %theta_v_hbm.1, bf16[3072,3072]{1,0:T(8,128)(2,1)} %theta_q_hbm.1, bf16[3072,3072]{1,0:T(8,128)(2,1)} %w_hbm.1, ...), custom_call_target="tpu_custom_call" | custom-call | tf_op jit(solution)/shard_map/fused/pallas_call | solution.py:493
  248.5 22.1 %rest.1 = bf16[2048,3072]{1,0:T(8,128)(2,1)} custom-call(bf16[2048,1280]{1,0:T(8,128)(2,1)} %bitcast.4, bf16[3072,3072]{1,0:T(8,128)(2,1)} %w_hbm.1, f32[12,4,8,64,256]{4,3,2,1,0:T(8,128)} %get-tuple-element.8.sum_hbm), custom_call_target="tpu_custom_call" | custom-call | tf_op jit(solution)/shard_map/rest/pallas_call | solution.py:508
